TPU v7x, 32 devices: a whole 2x2x4 slice. The times are simulated.
32 devices in a mesh: worker: 8 (over y, x, core), mp: 4 (over z).
Axes of the slice: x: 2, y: 2, z: 4, core: 2. Of those that a mesh axis runs over, the one named last changes fastest.
Arguments:
- gradients: float32 [8, 2097152], P('worker', 'mp'), may hold values from -100 to 100
- neighbours: int32 [8, 3], replicated, may hold values from 0 to 7, as said below
- winner: int32 [1], replicated, may hold values from 0 to 7
Outputs:
- scores: float32 [8], replicated
- aggregate: float32 [2097152], P(('mp', 'worker'))
Inputs may be any that keep to these rules, and one draw needn't show every extreme that they name: `neighbours`: row i lists 3 different workers, none of them equal to i.
All inputs are finite; a program needn't handle non-finite values.
Results may differ from a plain program's by a relative error of at most 0.0003.
Values may be sent and summed in bfloat16 or wider, within the bound.
No kernel may reach another device: no remote copies, remote signals or barrier semaphores. Data moves between devices by JAX's collectives and lax.ppermute only.
A program may use at most 64 MiB of HBM per device.

v0:
```python
import jax
import jax.numpy as jnp
from jax import lax
from jax.sharding import PartitionSpec as P


def from_root(block, axis, holder):
    block = jnp.where(lax.axis_index(axis) == holder, block, jnp.zeros_like(block))
    return lax.psum(block, axis)


def body(gradients, neighbours, winner):
    rounded = gradients.astype(jnp.bfloat16)
    workers = lax.axis_size("worker")
    own_index = lax.axis_index("worker")
    length = gradients.shape[1]
    columns = lax.all_to_all(rounded, "worker", split_axis=1, concat_axis=0, tiled=True)
    partial_value = lax.dot_general(
        columns, columns, (((1,), (1,)), ((), ())), preferred_element_type=jnp.float32
    )
    gram_matrix = lax.psum(partial_value, ("worker", "mp"))
    squares = jnp.diagonal(gram_matrix)
    distance = squares[:, None] + squares[None, :] - 2.0 * gram_matrix
    counts = jnp.sum(
        (neighbours[:, :, None] == jnp.arange(workers, dtype=jnp.int32)[None, None, :]).astype(
            jnp.float32
        ),
        axis=1,
    )
    total_entries = neighbours.shape[1] * length * lax.axis_size("mp")
    scores = jnp.sum(counts * distance, axis=1) / jnp.float32(total_entries)
    piece_length = length // workers
    selected = from_root(gradients[0], "worker", winner[0])
    aggregate = lax.dynamic_slice_in_dim(selected, own_index * piece_length, piece_length, 0)
    return (scores, aggregate)


def solution(mesh):
    in_specs = (P("worker", "mp"), P(), P())
    out_specs = (P(), P(("mp", "worker")))
    return jax.shard_map(body, mesh=mesh, in_specs=in_specs, out_specs=out_specs, check_vma=False)
```

profile of v0, /device:TPU:0, one launch (start us, length us, event | category | flops | bytes accessed | tf_op | source)
XLA Modules:
  0.0 107.3 jit_solution(818342998343869056)
XLA Ops:
  7.8 6.5 %broadcast_select_fusion = (f32[1,524288]{1,0:T(1,128)}, bf16[1,524288]{1,0:T(2,128)(2,1)S(1)}) fusion(f32[1,524288]{1,0:T(1,128)} %param.3, pred[]{:T(512)S(6)} %eq.19), kind=kLoop, calls=%fused_computation.1 | loop fusion | flops 1048576 | bytes 5242881 | tf_op jit(solution)/shard_map/jit(_where)/select_n | solution.py:8
  14.3 0.5 broadcast.34
  14.8 7.0 %reduce = bf16[8,65536]{1,0:T(8,128)(2,1)S(1)} reduce(bf16[8,1,65536]{2,1,0:T(2,128)(2,1)S(1)} %bitcast.12, bf16[]{:T(256)} %broadcast.34), dimensions={1}, to_apply=%bitcast.8.reduce_sub_computation | reduce | bytes 2097154
  21.9 1.9 %reshape.22 = bf16[8,2,32768]{2,1,0:T(2,128)(2,1)} reshape(bf16[8,65536]{1,0:T(8,128)(2,1)S(1)} %reduce) | data formatting | bytes 2097152
  23.7 0.0 copy-start
  23.7 5.3 %all-to-all-start = ((bf16[8,2,32768]{2,1,0:T(2,128)(2,1)}), bf16[8,2,32768]{2,1,0:T(2,128)(2,1)S(1)}, u32[]{:S(2)}, u32[]{:S(2)}) async-start(bf16[8,2,32768]{2,1,0:T(2,128)(2,1)} %reshape.22), calls=%async_computation | async-start | bytes 2097152 | tf_op jit(solution)/shard_map/all_to_all | solution.py:17
  29.1 0.0 all-reduce.2.cloned.1.call-start
  29.1 0.7 all-reduce.2.cloned.1.call-update
  29.8 0.0 copy-done
  29.8 0.1 convert_reduce_fusion
  29.9 16.4 %all-to-all-done = bf16[8,2,32768]{2,1,0:T(2,128)(2,1)S(1)} async-done(((bf16[8,2,32768]{2,1,0:T(2,128)(2,1)}), bf16[8,2,32768]{2,1,0:T(2,128)(2,1)S(1)}, u32[]{:S(2)}, u32[]{:S(2)}) %all-to-all-start) | async-done | bytes 1048608 | tf_op jit(solution)/shard_map/all_to_all | solution.py:17
  46.3 1.0 reshape.23
  47.3 1.2 %fusion = f32[8,8]{1,0:T(8,128)S(1)} fusion(bf16[1,8,65536]{2,0,1:T(2,128)(2,1)S(1)} %bitcast.13), kind=kOutput, calls=%fused_computation.2 | convolution fusion | flops 8388608 | bytes 1048832 | tf_op jit(solution)/shard_map/dot_general | solution.py:18
  48.5 39.8 %psum.14 = f32[8,8]{1,0:T(8,128)S(1)} all-reduce(f32[8,8]{1,0:T(8,128)S(1)} %fusion), channel_id=1, replica_groups=mesh['worker'=8,'mp'=4] {'worker','mp'}, use_global_device_ids=true, to_apply=%region_1.2 | all-reduce | flops 64 | bytes 512 | tf_op jit(solution)/shard_map/psum | solution.py:21
  88.3 0.6 gather_fusion
  88.9 0.2 multiply_reduce_fusion
  89.1 0.5 broadcast_multiply_fusion
  89.6 9.1 %all-reduce.2.cloned.1.call-done = f32[524288]{0:T(1024)} async-done(((f32[524288]{0:T(1024)}), f32[524288]{0:T(1024)}) %all-reduce.2.cloned.1.call-update) | async-done | bytes 2097168 | tf_op jit(solution)/shard_map/psum | solution.py:9
  98.8 1.7 %dynamic_slice.3 = f32[65536]{0:T(1024)} dynamic-slice(f32[524288]{0:T(1024)} %all-reduce.2.cloned.1.call-done, s32[]{:T(128)S(6)} %select_n.21), dynamic_slice_sizes={65536} | dynamic-slice | bytes 524292 | tf_op jit(solution)/shard_map/dynamic_slice | solution.py:34
  (1 shorter events, 0.0 us)
Async XLA Ops:
  23.7 6.1 %copy-start = (s32[8,3]{0,1:T(4,128)S(1)}, s32[8,3]{0,1:T(4,128)}, u32[]{:S(2)}) copy-start(s32[8,3]{0,1:T(4,128)} %param.4) | copy-start | bytes 292
  23.7 22.5 %all-to-all-start = ((bf16[8,2,32768]{2,1,0:T(2,128)(2,1)}), bf16[8,2,32768]{2,1,0:T(2,128)(2,1)S(1)}, u32[]{:S(2)}, u32[]{:S(2)}) async-start(bf16[8,2,32768]{2,1,0:T(2,128)(2,1)} %reshape.22), calls=%async_computation | async-start | bytes 2097152 | tf_op jit(solution)/shard_map/all_to_all | solution.py:17
  29.1 69.7 %all-reduce.2.cloned.1.call-start = ((), (), s32[]{:S(2)}) async-start(), calls=%async_computation.1 | async-start | bytes 4194304 | tf_op jit(solution)/shard_map/psum | solution.py:9
Sparse Core Ops, SparseCore 0:
  33.1 65.6 all-reduce.1
where the time goes:
time: 108 us; the launch traced here: 107 us
  blocking collectives  39.8 us (37%)
  waiting for transfers between devices  26.2 us (24%)
  between operations  14.7 us (14%)
  other arithmetic  14.3 us (13%)
  local copies, waits for them, and re-layouts  5.71 us (5%)
  starting transfers between devices  5.37 us (5%)
  matrix products  1.2 us (1%)
    psum x1, blocking collectives, body(): gram_matrix = lax.psum(partial_value, ('worker', 'mp'))  39.8 us
    all_to_all x1, waiting for transfers between devices, body(): lax.all_to_all(rounded, 'worker', split_axis=1, concat_axis=0, tiled=True)  16.4 us
    psum x1, waiting for transfers between devices, from_root(): return lax.psum(block, axis)  9.12 us
    unnamed x1, other arithmetic  7.03 us
    select_n x1, other arithmetic, from_root(): jnp.where(lax.axis_index(axis) == holder, block, jnp.zeros_like(block))  6.5 us
    all_to_all x1, starting transfers between devices, body(): lax.all_to_all(rounded, 'worker', split_axis=1, concat_axis=0, tiled=True)  5.33 us
    unnamed x5, local copies, waits for them, and re-layouts  3.41 us
  transfers between devices with their start and end apart: 2, of which 2 were waited for; matrix products, arithmetic and copies ran while one was open for 3% of the time, Pallas kernels for 0%

commit v1 on v0

v1 whole, which is shorter than its diff:
```python
import jax
import jax.numpy as jnp
from jax import lax
from jax.experimental import pallas as pl
from jax.experimental.pallas import tpu as pltpu
from jax.sharding import PartitionSpec as P

LANES = 128


def score_kernel(neighbours, columns, out, *, scale):
    workers, rows, lanes = columns.shape
    nbr = neighbours.shape[1]
    chunk = 16

    def step(r, accs):
        at = pl.ds(pl.multiple_of(r * chunk, chunk), chunk)
        new = []
        for i in range(workers):
            own = columns[i, at, :].astype(jnp.float32)
            acc = accs[i]
            for j in range(nbr):
                diff = own - columns[neighbours[i, j], at, :].astype(jnp.float32)
                square = diff * diff
                acc = acc + (square[:8] + square[8:])
            new.append(acc)
        return tuple(new)

    zero = jnp.zeros((8, lanes), jnp.float32)
    accs = lax.fori_loop(0, rows // chunk, step, (zero,) * workers)
    lane = lax.broadcasted_iota(jnp.int32, (1, lanes), 1)
    row = jnp.zeros((1, lanes), jnp.float32)
    for i in range(workers):
        total = jnp.sum(jnp.sum(accs[i], axis=0, keepdims=True), axis=1, keepdims=True)
        row = jnp.where(lane == i, total * scale, row)
    out[...] = jnp.broadcast_to(row[None], out.shape)


def partial_scores(neighbours, columns, devices, scale):
    def kernel(n, c, o):
        score_kernel(n, c, o, scale=scale)

    return pl.pallas_call(
        kernel,
        out_shape=jax.ShapeDtypeStruct((devices, 1, LANES), jnp.float32),
        in_specs=[
            pl.BlockSpec(memory_space=pltpu.SMEM),
            pl.BlockSpec(memory_space=pltpu.VMEM),
        ],
        out_specs=pl.BlockSpec(memory_space=pltpu.VMEM),
        name="scores",
    )(neighbours, columns)


def low_part(x):
    return (x - lax.reduce_precision(x, 8, 7)).astype(jnp.bfloat16)


def body(gradients, neighbours, winner):
    workers = lax.axis_size("worker")
    devices = workers * lax.axis_size("mp")
    me = lax.axis_index("worker")
    length = gradients.shape[1]
    rows = length // workers // LANES
    pieces = gradients.reshape(workers, rows, LANES)
    columns = lax.all_to_all(
        pieces.astype(jnp.bfloat16), "worker", split_axis=0, concat_axis=0, tiled=True
    )
    scale = 1.0 / float(neighbours.shape[1] * length * lax.axis_size("mp"))
    partial_value = partial_scores(neighbours, columns, devices, scale)
    everyone = lax.all_to_all(
        partial_value, ("worker", "mp"), split_axis=0, concat_axis=0, tiled=True
    )
    scores = jnp.sum(everyone, axis=0)[0, :workers]

    chips = workers // 2
    chip, core = me // 2, me % 2
    best = winner[0]
    halves = pieces.reshape(chips, 2, rows, LANES)
    keep = lax.dynamic_index_in_dim(halves, core, 1, keepdims=False)
    give = lax.dynamic_index_in_dim(halves, 1 - core, 1, keepdims=False)
    got = lax.ppermute(low_part(give), "worker", [(i, i ^ 1) for i in range(workers)])
    mine = jnp.where(best % 2 == core, low_part(keep), got)
    low = lax.dynamic_index_in_dim(mine, chip, 0, keepdims=False)
    for d in range(1, chips):
        sent = lax.dynamic_index_in_dim(mine, chip ^ d, 0, keepdims=False)
        came = lax.ppermute(sent, "worker", [(i, i ^ (2 * d)) for i in range(workers)])
        low = jnp.where(best // 2 == chip ^ d, came, low)
    high = lax.dynamic_index_in_dim(columns, best, 0, keepdims=False)
    aggregate = high.astype(jnp.float32) + low.astype(jnp.float32)
    return (scores, aggregate.reshape(-1))


def solution(mesh):
    in_specs = (P("worker", "mp"), P(), P())
    out_specs = (P(), P(("mp", "worker")))
    return jax.shard_map(body, mesh=mesh, in_specs=in_specs, out_specs=out_specs, check_vma=False)
```

time: 108 us -> 64.4 us (0.60)
  blocking collectives: 39.8 us -> 0 us
  other arithmetic: 14.3 us -> 27.9 us
  between operations: 14.7 us -> 1.44 us
  waiting for transfers between devices: 26.2 us -> 15.4 us
  starting transfers between devices: 5.37 us -> 13.1 us
  Pallas kernels: 0 us -> 3.27 us
  local copies, waits for them, and re-layouts: 5.71 us -> 2.99 us
  matrix products: 1.2 us -> 0 us
    psum x1 -> x0, blocking collectives: 39.8 us -> none  [body(): gram_matrix = lax.psum(partial_value, ('worker', 'mp'))]
    convert_element_type x0 -> x2, other arithmetic: none -> 25.9 us  [the longest x1 23.7 us: body(): pieces.astype(jnp.bfloat16)]
    psum x1 -> x0, waiting for transfers between devices: 9.12 us -> none  [from_root(): return lax.psum(block, axis)]
    unnamed x1 -> x0, other arithmetic: 7.03 us -> none
    select_n x1, other arithmetic: 6.5 us -> 0.18 us  [body(): mine = jnp.where(best % 2 == core, low_part(keep), got)]
    ppermute x0 -> x4, starting transfers between devices: none -> 4.12 us  [the longest x3 3.63 us: body(): lax.ppermute(sent, 'worker', [(i, i ^ 2 * d) for i in range(workers)])]
    all_to_all x1 -> x2, starting transfers between devices: 5.33 us -> 8.93 us  [the longest x1 4.96 us: body(): lax.all_to_all(pieces.astype(jnp.bfloat16), 'worker', split_axis=0, conca...]
    pallas_call x0 -> x1, Pallas kernels: none -> 3.27 us  [partial_scores(): pl.pallas_call(kernel, out_shape=jax.ShapeDtypeStruct((devices, 1, LANES)...]
  transfers between devices with their start and end apart: 2 -> 6, of which waited for: 2 -> 2; matrix products, arithmetic and copies ran while one was open for 3% -> 41% of each run, Pallas kernels for 0% -> 5%
where the time goes in v1:
time: 64.4 us; the launch traced here: 64.1 us
  other arithmetic  27.9 us (43%)
  waiting for transfers between devices  15.4 us (24%)
  starting transfers between devices  13.1 us (20%)
  Pallas kernels  3.27 us (5%)
  local copies, waits for them, and re-layouts  2.99 us (5%)
  between operations  1.44 us (2%)
    convert_element_type x1, other arithmetic, body(): pieces.astype(jnp.bfloat16)  23.7 us
    all_to_all x1, waiting for transfers between devices, body(): lax.all_to_all(pieces.astype(jnp.bfloat16), 'worker', split_axis=0, conca...  9.97 us
    all_to_all x1, waiting for transfers between devices, body(): lax.all_to_all(partial_value, ('worker', 'mp'), split_axis=0, concat_axis...  5.45 us
    all_to_all x1, starting transfers between devices, body(): lax.all_to_all(pieces.astype(jnp.bfloat16), 'worker', split_axis=0, conca...  4.96 us
    all_to_all x1, starting transfers between devices, body(): lax.all_to_all(partial_value, ('worker', 'mp'), split_axis=0, concat_axis...  3.97 us
    ppermute x3, starting transfers between devices, body(): lax.ppermute(sent, 'worker', [(i, i ^ 2 * d) for i in range(workers)])  3.63 us
    pallas_call x1, Pallas kernels, partial_scores(): pl.pallas_call(kernel, out_shape=jax.ShapeDtypeStruct((devices, 1, LANES)...  3.27 us
    unnamed x9, local copies, waits for them, and re-layouts  2.45 us
  transfers between devices with their start and end apart: 6, of which 2 were waited for; matrix products, arithmetic and copies ran while one was open for 41% of the time, Pallas kernels for 5%

profile of v1, /device:TPU:0, one launch (start us, length us, event | category | flops | bytes accessed | tf_op | source)
XLA Modules:
  0.0 64.1 jit_solution(1246220039125392950)
XLA Ops:
  0.6 2.2 %fusion.1 = bf16[4,512,128]{2,1,0:T(8,128)(2,1)} fusion(f32[4,2,512,128]{3,2,1,0:T(8,128)} %bitcast.37, s32[]{:T(128)S(6)} %select_n.80), kind=kLoop, calls=%fused_computation.4 | loop fusion | flops 786432 | bytes 1572868 | tf_op jit(solution)/shard_map/convert_element_type | solution.py:56
  2.8 0.0 copy-start
  2.8 0.5 collective-permute-start
  3.3 23.7 %convert_reduce_fusion = bf16[524288]{0:T(1024)(128)(2,1)} fusion(f32[1,524288]{1,0:T(1,128)} %param.3), kind=kLoop, calls=%fused_computation | loop fusion | flops 524288 | bytes 3145728 | tf_op jit(solution)/shard_map/convert_element_type | solution.py:67
  27.1 0.0 copy-start.3
  27.1 5.0 %all-to-all-start = ((bf16[8,512,128]{2,1,0:T(8,128)(2,1)}), bf16[8,512,128]{2,1,0:T(8,128)(2,1)S(1)}, u32[]{:S(2)}, u32[]{:S(2)}) async-start(bf16[8,512,128]{2,1,0:T(8,128)(2,1)} %bitcast.39), calls=%async_computation | async-start | bytes 2097152 | tf_op jit(solution)/shard_map/all_to_all | solution.py:66
  32.7 0.0 collective-permute-done
  32.7 0.0 copy-done
  32.8 0.2 fusion.2
  33.0 0.0 copy-start.2
  33.0 0.8 %copy-done.2 = bf16[4,512,128]{2,1,0:T(8,128)(2,1)} copy-done((bf16[4,512,128]{2,1,0:T(8,128)(2,1)}, bf16[4,512,128]{2,1,0:T(8,128)(2,1)S(1)}, u32[]{:S(2)}) %copy-start.2) | copy-done | bytes 524312
  33.8 3.0 %collective-permute-start.1 = (bf16[512,128]{1,0:T(8,128)(2,1)S(1)}, bf16[512,128]{1,0:T(8,128)(2,1)S(1)}, u32[]{:S(2)}, u32[]{:S(2)}) collective-permute-start(bf16[512,128]{1,0:T(8,128)(2,1)S(1)} %get-tuple-element.4), channel_id=1, source_target_pairs={{0,24},{4,28},{8,16},{12,20},{16,8},{20,12},{24,0},{28,4},{1,25},{... | collective-permute-start | bytes 393224 | tf_op jit(solution)/shard_map/ppermute | solution.py:87
  36.8 0.6 collective-permute-start.2
  37.3 0.1 collective-permute-start.3
  37.4 0.0 copy-done.3
  37.4 0.7 %copy.5.n = s32[8,3]{1,0:T(8,128)} copy(s32[8,3]{0,1:T(4,128)S(1)} %copy-done.3) | data formatting | bytes 192 | tf_op args[1]
  38.1 10.0 %all-to-all-done.c = bf16[8,512,128]{2,1,0:T(8,128)(2,1)S(1)} async-done(((bf16[8,512,128]{2,1,0:T(8,128)(2,1)}), bf16[8,512,128]{2,1,0:T(8,128)(2,1)S(1)}, u32[]{:S(2)}, u32[]{:S(2)}) %all-to-all-start) | async-done | bytes 1048608 | tf_op jit(solution)/shard_map/all_to_all | solution.py:66
  48.1 0.0 copy-start.1
  48.1 1.0 %copy-done.1 = bf16[8,512,128]{2,1,0:T(8,128)(2,1)} copy-done((bf16[8,512,128]{2,1,0:T(8,128)(2,1)}, bf16[8,512,128]{2,1,0:T(8,128)(2,1)S(1)}, u32[]{:S(2)}) %copy-start.1) | copy-done | bytes 1048600
  49.0 3.3 %scores.1 = f32[32,1,128]{2,1,0:T(1,128)} custom-call(s32[8,3]{1,0:T(8,128)} %copy.5.n, bf16[8,512,128]{2,1,0:T(8,128)(2,1)} %copy-done.1), custom_call_target="tpu_custom_call" | custom-call | tf_op jit(solution)/shard_map/scores/pallas_call | solution.py:43
  52.3 4.0 %all-to-all-start.1 = ((f32[32,1,128]{2,1,0:T(1,128)}), f32[32,1,128]{2,1,0:T(1,128)S(1)}, u32[]{:S(2)}, u32[]{:S(2)}) async-start(f32[32,1,128]{2,1,0:T(1,128)} %scores.1), calls=%async_computation.1 | async-start | bytes 32768 | tf_op jit(solution)/shard_map/all_to_all | solution.py:71
  56.3 0.0 collective-permute-done.1
  56.3 0.0 collective-permute-done.2
  56.3 0.0 collective-permute-done.3
  56.3 1.7 %fusion.3 = f32[65536]{0:T(1024)} fusion(bf16[512,128]{1,0:T(8,128)(2,1)S(1)} %collective-permute-done.1, bf16[512,128]{1,0:T(8,128)(2,1)S(1)} %collective-permute-done.2, bf16[512,128]{1,0:T(8,128)(2,1)S(1)} %collective-permute-done.3, bf16[4,512,128]{2,1,0:T(8,128)(2,1)} %copy-done.2, s32[]{:T(128)S(6)} %select_n.87, bf16[8,512,128]{2,1,0:T(8,128)(2,1)} %copy-done.1, ...), kind=kLoop, calls=%fused_computation.7 | loop fusion | flops 393216 | bytes 917515 | tf_op jit(solution)/shard_map/reshape | solution.py:91
  58.0 5.4 %all-to-all-done.1 = f32[32,1,128]{2,1,0:T(1,128)S(1)} async-done(((f32[32,1,128]{2,1,0:T(1,128)}), f32[32,1,128]{2,1,0:T(1,128)S(1)}, u32[]{:S(2)}, u32[]{:S(2)}) %all-to-all-start.1) | async-done | bytes 16416 | tf_op jit(solution)/shard_map/all_to_all | solution.py:71
  63.5 0.1 reduce_sum.11
  63.5 0.5 slice_bitcast_fusion
  (1 shorter events, 0.0 us)
Async XLA Ops:
  2.8 29.9 %copy-start = (f32[1,524288]{1,0:T(1,128)S(1)}, f32[1,524288]{1,0:T(1,128)}, u32[]{:S(2)}) copy-start(f32[1,524288]{1,0:T(1,128)} %param.3) | copy-start | bytes 6291460
  2.8 29.9 %collective-permute-start = (bf16[4,512,128]{2,1,0:T(8,128)(2,1)}, bf16[4,512,128]{2,1,0:T(8,128)(2,1)}, u32[]{:S(2)}, u32[]{:S(2)}) collective-permute-start(bf16[4,512,128]{2,1,0:T(8,128)(2,1)} %fusion.1), channel_id=1, source_target_pairs={{0,4},{4,0},{8,12},{12,8},{16,20},{20,16},{24,28},{28,24},{1,5},{5... | collective-permute-start | bytes 1572872 | tf_op jit(solution)/shard_map/ppermute | solution.py:82
  27.1 10.4 %copy-start.3 = (s32[8,3]{0,1:T(4,128)S(1)}, s32[8,3]{0,1:T(4,128)}, u32[]{:S(2)}) copy-start(s32[8,3]{0,1:T(4,128)} %param.4) | copy-start | bytes 292
  27.1 21.0 %all-to-all-start = ((bf16[8,512,128]{2,1,0:T(8,128)(2,1)}), bf16[8,512,128]{2,1,0:T(8,128)(2,1)S(1)}, u32[]{:S(2)}, u32[]{:S(2)}) async-start(bf16[8,512,128]{2,1,0:T(8,128)(2,1)} %bitcast.39), calls=%async_computation | async-start | bytes 2097152 | tf_op jit(solution)/shard_map/all_to_all | solution.py:66
  33.0 0.8 %copy-start.2 = (bf16[4,512,128]{2,1,0:T(8,128)(2,1)}, bf16[4,512,128]{2,1,0:T(8,128)(2,1)S(1)}, u32[]{:S(2)}) copy-start(bf16[4,512,128]{2,1,0:T(8,128)(2,1)S(1)} %fusion.2) | copy-start | bytes 1572868
  33.8 22.5 %collective-permute-start.1 = (bf16[512,128]{1,0:T(8,128)(2,1)S(1)}, bf16[512,128]{1,0:T(8,128)(2,1)S(1)}, u32[]{:S(2)}, u32[]{:S(2)}) collective-permute-start(bf16[512,128]{1,0:T(8,128)(2,1)S(1)} %get-tuple-element.4), channel_id=1, source_target_pairs={{0,24},{4,28},{8,16},{12,20},{16,8},{20,12},{24,0},{28,4},{1,25},{... | collective-permute-start | bytes 393224 | tf_op jit(solution)/shard_map/ppermute | solution.py:87
  36.8 19.5 %collective-permute-start.2 = (bf16[512,128]{1,0:T(8,128)(2,1)S(1)}, bf16[512,128]{1,0:T(8,128)(2,1)S(1)}, u32[]{:S(2)}, u32[]{:S(2)}) collective-permute-start(bf16[512,128]{1,0:T(8,128)(2,1)S(1)} %get-tuple-element.3), channel_id=1, source_target_pairs={{0,16},{4,20},{8,24},{12,28},{16,0},{20,4},{24,8},{28,12},{1,17},{... | collective-permute-start | bytes 393224 | tf_op jit(solution)/shard_map/ppermute | solution.py:87
  37.3 19.0 %collective-permute-start.3 = (bf16[512,128]{1,0:T(8,128)(2,1)S(1)}, bf16[512,128]{1,0:T(8,128)(2,1)S(1)}, u32[]{:S(2)}, u32[]{:S(2)}) collective-permute-start(bf16[512,128]{1,0:T(8,128)(2,1)S(1)} %get-tuple-element.2), channel_id=1, source_target_pairs={{0,8},{4,12},{8,0},{12,4},{16,24},{20,28},{24,16},{28,20},{1,9},{5... | collective-permute-start | bytes 393224 | tf_op jit(solution)/shard_map/ppermute | solution.py:87
  48.1 1.0 %copy-start.1 = (bf16[8,512,128]{2,1,0:T(8,128)(2,1)}, bf16[8,512,128]{2,1,0:T(8,128)(2,1)S(1)}, u32[]{:S(2)}) copy-start(bf16[8,512,128]{2,1,0:T(8,128)(2,1)S(1)} %all-to-all-done.c) | copy-start | bytes 3145732
  52.3 11.2 %all-to-all-start.1 = ((f32[32,1,128]{2,1,0:T(1,128)}), f32[32,1,128]{2,1,0:T(1,128)S(1)}, u32[]{:S(2)}, u32[]{:S(2)}) async-start(f32[32,1,128]{2,1,0:T(1,128)} %scores.1), calls=%async_computation.1 | async-start | bytes 32768 | tf_op jit(solution)/shard_map/all_to_all | solution.py:71

commit v2 on v1

--- a/solution.py
+++ b/solution.py
@@ -52,8 +52,41 @@
     )(neighbours, columns)
 
 
-def low_part(x):
-    return (x - lax.reduce_precision(x, 8, 7)).astype(jnp.bfloat16)
+def split_kernel(core, pieces, high, give, keep):
+    value = pieces[0]
+    rounded = value.astype(jnp.bfloat16)
+    high[0] = rounded
+    low = (value - rounded.astype(jnp.float32)).astype(jnp.bfloat16)
+    mine = core[0] == pl.program_id(0) % 2
+
+    @pl.when(mine)
+    def _():
+        keep[0] = low
+
+    @pl.when(jnp.logical_not(mine))
+    def _():
+        give[0] = low
+
+
+def split(core, pieces):
+    workers, rows, lanes = pieces.shape
+    block = (1, rows, lanes)
+    half = jax.ShapeDtypeStruct((workers // 2, rows, lanes), jnp.bfloat16)
+    return pl.pallas_call(
+        split_kernel,
+        grid=(workers,),
+        out_shape=(jax.ShapeDtypeStruct(pieces.shape, jnp.bfloat16), half, half),
+        in_specs=[
+            pl.BlockSpec(memory_space=pltpu.SMEM),
+            pl.BlockSpec(block, lambda i: (i, 0, 0)),
+        ],
+        out_specs=(
+            pl.BlockSpec(block, lambda i: (i, 0, 0)),
+            pl.BlockSpec(block, lambda i: (i // 2, 0, 0)),
+            pl.BlockSpec(block, lambda i: (i // 2, 0, 0)),
+        ),
+        name="split",
+    )(core, pieces)
 
 
 def body(gradients, neighbours, winner):
@@ -63,9 +96,9 @@
     length = gradients.shape[1]
     rows = length // workers // LANES
     pieces = gradients.reshape(workers, rows, LANES)
-    columns = lax.all_to_all(
-        pieces.astype(jnp.bfloat16), "worker", split_axis=0, concat_axis=0, tiled=True
-    )
+    core = me & 1
+    high, give, keep = split(core.reshape(1), pieces)
+    columns = lax.all_to_all(high, "worker", split_axis=0, concat_axis=0, tiled=True)
     scale = 1.0 / float(neighbours.shape[1] * length * lax.axis_size("mp"))
     partial_value = partial_scores(neighbours, columns, devices, scale)
     everyone = lax.all_to_all(
@@ -74,20 +107,17 @@
     scores = jnp.sum(everyone, axis=0)[0, :workers]
 
     chips = workers // 2
-    chip, core = me // 2, me % 2
+    chip = me >> 1
     best = winner[0]
-    halves = pieces.reshape(chips, 2, rows, LANES)
-    keep = lax.dynamic_index_in_dim(halves, core, 1, keepdims=False)
-    give = lax.dynamic_index_in_dim(halves, 1 - core, 1, keepdims=False)
-    got = lax.ppermute(low_part(give), "worker", [(i, i ^ 1) for i in range(workers)])
-    mine = jnp.where(best % 2 == core, low_part(keep), got)
+    got = lax.ppermute(give, "worker", [(i, i ^ 1) for i in range(workers)])
+    mine = jnp.where((best & 1) == core, keep, got)
     low = lax.dynamic_index_in_dim(mine, chip, 0, keepdims=False)
     for d in range(1, chips):
         sent = lax.dynamic_index_in_dim(mine, chip ^ d, 0, keepdims=False)
         came = lax.ppermute(sent, "worker", [(i, i ^ (2 * d)) for i in range(workers)])
-        low = jnp.where(best // 2 == chip ^ d, came, low)
-    high = lax.dynamic_index_in_dim(columns, best, 0, keepdims=False)
-    aggregate = high.astype(jnp.float32) + low.astype(jnp.float32)
+        low = jnp.where(best >> 1 == chip ^ d, came, low)
+    rounded = lax.dynamic_index_in_dim(columns, best, 0, keepdims=False)
+    aggregate = rounded.astype(jnp.float32) + low.astype(jnp.float32)
     return (scores, aggregate.reshape(-1))
 
 

time: 64.4 us -> 44.3 us (0.69)
  other arithmetic: 27.9 us -> 1.77 us
  Pallas kernels: 3.27 us -> 9.04 us
  waiting for transfers between devices: 15.4 us -> 16.5 us
  local copies, waits for them, and re-layouts: 2.99 us -> 2.21 us
    convert_element_type x2 -> x0, other arithmetic: 25.9 us -> none  [the longest x1 23.7 us: body(): pieces.astype(jnp.bfloat16)]
    pallas_call x0 -> x1, Pallas kernels: none -> 5.76 us  [split(): pl.pallas_call(split_kernel, grid=(workers,), out_shape=(jax.ShapeDtypeSt...]
    all_to_all x1, waiting for transfers between devices: 9.97 us -> 10.9 us  [body(): lax.all_to_all(high, 'worker', split_axis=0, concat_axis=0, tiled=True)]
    unnamed x9 -> x7, local copies, waits for them, and re-layouts: 2.45 us -> 1.65 us
  transfers between devices with their start and end apart: 6 -> 6, of which waited for: 2 -> 2; matrix products, arithmetic and copies ran while one was open for 41% -> 6% of each run, Pallas kernels for 5% -> 7%
where the time goes in v2:
time: 44.3 us; the launch traced here: 43.9 us
  waiting for transfers between devices  16.5 us (37%)
  starting transfers between devices  13 us (29%)
  Pallas kernels  9.04 us (20%)
  local copies, waits for them, and re-layouts  2.21 us (5%)
  other arithmetic  1.77 us (4%)
  between operations  1.37 us (3%)
    all_to_all x1, waiting for transfers between devices, body(): lax.all_to_all(high, 'worker', split_axis=0, concat_axis=0, tiled=True)  10.9 us
    pallas_call x1, Pallas kernels, split(): pl.pallas_call(split_kernel, grid=(workers,), out_shape=(jax.ShapeDtypeSt...  5.76 us
    all_to_all x1, waiting for transfers between devices, body(): lax.all_to_all(partial_value, ('worker', 'mp'), split_axis=0, concat_axis...  5.51 us
    all_to_all x1, starting transfers between devices, body(): lax.all_to_all(high, 'worker', split_axis=0, concat_axis=0, tiled=True)  4.98 us
    all_to_all x1, starting transfers between devices, body(): lax.all_to_all(partial_value, ('worker', 'mp'), split_axis=0, concat_axis...  3.97 us
    ppermute x3, starting transfers between devices, body(): lax.ppermute(sent, 'worker', [(i, i ^ 2 * d) for i in range(workers)])  3.63 us
    pallas_call x1, Pallas kernels, partial_scores(): pl.pallas_call(kernel, out_shape=jax.ShapeDtypeStruct((devices, 1, LANES)...  3.28 us
    reshape x1, other arithmetic, body(): return (scores, aggregate.reshape(-1))  1.66 us
  transfers between devices with their start and end apart: 6, of which 2 were waited for; matrix products, arithmetic and copies ran while one was open for 6% of the time, Pallas kernels for 7%

profile of v2, /device:TPU:0, one launch (start us, length us, event | category | flops | bytes accessed | tf_op | source)
XLA Modules:
  0.0 43.9 jit_solution(5346991888561652326)
XLA Ops:
  0.6 5.8 %split.1 = (bf16[8,512,128]{2,1,0:T(8,128)(2,1)}, bf16[4,512,128]{2,1,0:T(8,128)(2,1)}, bf16[4,512,128]{2,1,0:T(8,128)(2,1)}) custom-call(s32[1]{0:T(128)} %bitcast.core, f32[8,512,128]{2,1,0:T(8,128)} %bitcast.30), custom_call_target="tpu_custom_call" | custom-call | tf_op jit(solution)/shard_map/split/pallas_call | solution.py:75
  6.4 0.0 copy-start.1
  6.4 0.5 %collective-permute-start = (bf16[4,512,128]{2,1,0:T(8,128)(2,1)}, bf16[4,512,128]{2,1,0:T(8,128)(2,1)S(1)}, u32[]{:S(2)}, u32[]{:S(2)}) collective-permute-start(bf16[4,512,128]{2,1,0:T(8,128)(2,1)} %get-tuple-element.7), channel_id=1, source_target_pairs={{0,4},{4,0},{8,12},{12,8},{16,20},{20,16},{24,28},{28,24},{1,5},{5... | collective-permute-start | bytes 1572872 | tf_op jit(solution)/shard_map/ppermute | solution.py:112
  6.9 0.0 copy-start.2
  6.9 5.0 %all-to-all-start = ((bf16[8,512,128]{2,1,0:T(8,128)(2,1)}), bf16[8,512,128]{2,1,0:T(8,128)(2,1)S(1)}, u32[]{:S(2)}, u32[]{:S(2)}) async-start(bf16[8,512,128]{2,1,0:T(8,128)(2,1)} %get-tuple-element.5), calls=%async_computation | async-start | bytes 2097152 | tf_op jit(solution)/shard_map/all_to_all | solution.py:101
  12.5 0.0 collective-permute-done
  12.5 0.0 copy-done.1
  12.5 0.1 broadcast_select_fusion
  12.6 3.0 %collective-permute-start.1 = (bf16[512,128]{1,0:T(8,128)(2,1)S(1)}, bf16[512,128]{1,0:T(8,128)(2,1)S(1)}, u32[]{:S(2)}, u32[]{:S(2)}) collective-permute-start(bf16[512,128]{1,0:T(8,128)(2,1)S(1)} %get-tuple-element.10), channel_id=1, source_target_pairs={{0,24},{4,28},{8,16},{12,20},{16,8},{20,12},{24,0},{28,4},{1,25},{... | collective-permute-start | bytes 393224 | tf_op jit(solution)/shard_map/ppermute | solution.py:117
  15.6 0.6 %collective-permute-start.2 = (bf16[512,128]{1,0:T(8,128)(2,1)S(1)}, bf16[512,128]{1,0:T(8,128)(2,1)S(1)}, u32[]{:S(2)}, u32[]{:S(2)}) collective-permute-start(bf16[512,128]{1,0:T(8,128)(2,1)S(1)} %get-tuple-element.9), channel_id=1, source_target_pairs={{0,16},{4,20},{8,24},{12,28},{16,0},{20,4},{24,8},{28,12},{1,17},{... | collective-permute-start | bytes 393224 | tf_op jit(solution)/shard_map/ppermute | solution.py:117
  16.2 0.1 collective-permute-start.3
  16.3 0.0 copy-done.2
  16.3 0.7 %copy.5.n = s32[8,3]{1,0:T(8,128)} copy(s32[8,3]{0,1:T(4,128)S(1)} %copy-done.2) | data formatting | bytes 192 | tf_op args[1]
  17.0 10.9 %all-to-all-done.c = bf16[8,512,128]{2,1,0:T(8,128)(2,1)S(1)} async-done(((bf16[8,512,128]{2,1,0:T(8,128)(2,1)}), bf16[8,512,128]{2,1,0:T(8,128)(2,1)S(1)}, u32[]{:S(2)}, u32[]{:S(2)}) %all-to-all-start) | async-done | bytes 1048608 | tf_op jit(solution)/shard_map/all_to_all | solution.py:101
  27.9 0.0 copy-start
  27.9 1.0 %copy-done = bf16[8,512,128]{2,1,0:T(8,128)(2,1)} copy-done((bf16[8,512,128]{2,1,0:T(8,128)(2,1)}, bf16[8,512,128]{2,1,0:T(8,128)(2,1)S(1)}, u32[]{:S(2)}) %copy-start) | copy-done | bytes 1048600
  28.9 3.3 %scores.1 = f32[32,1,128]{2,1,0:T(1,128)} custom-call(s32[8,3]{1,0:T(8,128)} %copy.5.n, bf16[8,512,128]{2,1,0:T(8,128)(2,1)} %copy-done), custom_call_target="tpu_custom_call" | custom-call | tf_op jit(solution)/shard_map/scores/pallas_call | solution.py:43
  32.2 4.0 %all-to-all-start.1 = ((f32[32,1,128]{2,1,0:T(1,128)}), f32[32,1,128]{2,1,0:T(1,128)S(1)}, u32[]{:S(2)}, u32[]{:S(2)}) async-start(f32[32,1,128]{2,1,0:T(1,128)} %scores.1), calls=%async_computation.1 | async-start | bytes 32768 | tf_op jit(solution)/shard_map/all_to_all | solution.py:104
  36.1 0.0 collective-permute-done.1
  36.1 0.0 collective-permute-done.2
  36.2 0.0 collective-permute-done.3
  36.2 1.7 %fusion = f32[65536]{0:T(1024)} fusion(bf16[512,128]{1,0:T(8,128)(2,1)S(1)} %collective-permute-done.1, bf16[512,128]{1,0:T(8,128)(2,1)S(1)} %collective-permute-done.2, bf16[512,128]{1,0:T(8,128)(2,1)S(1)} %collective-permute-done.3, bf16[4,512,128]{2,1,0:T(8,128)(2,1)S(1)} %broadcast_select_fusion, s32[]{:T(128)S(6)} %select_n.54, ...), kind=kLoop, calls=%fused_computation.2 | loop fusion | flops 393216 | bytes 917515 | tf_op jit(solution)/shard_map/reshape | solution.py:121
  37.8 5.5 %all-to-all-done.1 = f32[32,1,128]{2,1,0:T(1,128)S(1)} async-done(((f32[32,1,128]{2,1,0:T(1,128)}), f32[32,1,128]{2,1,0:T(1,128)S(1)}, u32[]{:S(2)}, u32[]{:S(2)}) %all-to-all-start.1) | async-done | bytes 16416 | tf_op jit(solution)/shard_map/all_to_all | solution.py:104
  43.3 0.1 reduce_sum.11
  43.4 0.5 %slice_bitcast_fusion = f32[8]{0:T(128)} fusion(f32[1,128]{1,0:T(1,128)S(1)} %bitcast.31), kind=kLoop, calls=%fused_computation.9 | loop fusion | bytes 64 | tf_op jit(solution)/shard_map/squeeze | solution.py:107
  (1 shorter events, 0.0 us)
Async XLA Ops:
  6.4 6.1 %copy-start.1 = (bf16[4,512,128]{2,1,0:T(8,128)(2,1)S(1)}, bf16[4,512,128]{2,1,0:T(8,128)(2,1)}, u32[]{:S(2)}) copy-start(bf16[4,512,128]{2,1,0:T(8,128)(2,1)} %get-tuple-element.6) | copy-start | bytes 1572868
  6.4 6.1 %collective-permute-start = (bf16[4,512,128]{2,1,0:T(8,128)(2,1)}, bf16[4,512,128]{2,1,0:T(8,128)(2,1)S(1)}, u32[]{:S(2)}, u32[]{:S(2)}) collective-permute-start(bf16[4,512,128]{2,1,0:T(8,128)(2,1)} %get-tuple-element.7), channel_id=1, source_target_pairs={{0,4},{4,0},{8,12},{12,8},{16,20},{20,16},{24,28},{28,24},{1,5},{5... | collective-permute-start | bytes 1572872 | tf_op jit(solution)/shard_map/ppermute | solution.py:112
  6.9 9.4 %copy-start.2 = (s32[8,3]{0,1:T(4,128)S(1)}, s32[8,3]{0,1:T(4,128)}, u32[]{:S(2)}) copy-start(s32[8,3]{0,1:T(4,128)} %param.4) | copy-start | bytes 292
  6.9 21.0 %all-to-all-start = ((bf16[8,512,128]{2,1,0:T(8,128)(2,1)}), bf16[8,512,128]{2,1,0:T(8,128)(2,1)S(1)}, u32[]{:S(2)}, u32[]{:S(2)}) async-start(bf16[8,512,128]{2,1,0:T(8,128)(2,1)} %get-tuple-element.5), calls=%async_computation | async-start | bytes 2097152 | tf_op jit(solution)/shard_map/all_to_all | solution.py:101
  12.6 23.5 %collective-permute-start.1 = (bf16[512,128]{1,0:T(8,128)(2,1)S(1)}, bf16[512,128]{1,0:T(8,128)(2,1)S(1)}, u32[]{:S(2)}, u32[]{:S(2)}) collective-permute-start(bf16[512,128]{1,0:T(8,128)(2,1)S(1)} %get-tuple-element.10), channel_id=1, source_target_pairs={{0,24},{4,28},{8,16},{12,20},{16,8},{20,12},{24,0},{28,4},{1,25},{... | collective-permute-start | bytes 393224 | tf_op jit(solution)/shard_map/ppermute | solution.py:117
  15.6 20.5 %collective-permute-start.2 = (bf16[512,128]{1,0:T(8,128)(2,1)S(1)}, bf16[512,128]{1,0:T(8,128)(2,1)S(1)}, u32[]{:S(2)}, u32[]{:S(2)}) collective-permute-start(bf16[512,128]{1,0:T(8,128)(2,1)S(1)} %get-tuple-element.9), channel_id=1, source_target_pairs={{0,16},{4,20},{8,24},{12,28},{16,0},{20,4},{24,8},{28,12},{1,17},{... | collective-permute-start | bytes 393224 | tf_op jit(solution)/shard_map/ppermute | solution.py:117
  16.2 20.0 %collective-permute-start.3 = (bf16[512,128]{1,0:T(8,128)(2,1)S(1)}, bf16[512,128]{1,0:T(8,128)(2,1)S(1)}, u32[]{:S(2)}, u32[]{:S(2)}) collective-permute-start(bf16[512,128]{1,0:T(8,128)(2,1)S(1)} %get-tuple-element.8), channel_id=1, source_target_pairs={{0,8},{4,12},{8,0},{12,4},{16,24},{20,28},{24,16},{28,20},{1,9},{5... | collective-permute-start | bytes 393224 | tf_op jit(solution)/shard_map/ppermute | solution.py:117
  27.9 1.0 %copy-start = (bf16[8,512,128]{2,1,0:T(8,128)(2,1)}, bf16[8,512,128]{2,1,0:T(8,128)(2,1)S(1)}, u32[]{:S(2)}) copy-start(bf16[8,512,128]{2,1,0:T(8,128)(2,1)S(1)} %all-to-all-done.c) | copy-start | bytes 3145732
  32.2 11.2 %all-to-all-start.1 = ((f32[32,1,128]{2,1,0:T(1,128)}), f32[32,1,128]{2,1,0:T(1,128)S(1)}, u32[]{:S(2)}, u32[]{:S(2)}) async-start(f32[32,1,128]{2,1,0:T(1,128)} %scores.1), calls=%async_computation.1 | async-start | bytes 32768 | tf_op jit(solution)/shard_map/all_to_all | solution.py:104

commit v3 on v0

v3 whole, which is shorter than its diff:
```python
import jax
import jax.numpy as jnp
from jax import lax
from jax.experimental import pallas as pl
from jax.experimental.pallas import tpu as pltpu
from jax.sharding import PartitionSpec as P

LANES = 128


def on_chip(x):
    return pltpu.with_memory_space_constraint(x, pltpu.VMEM)


def exchange(x, step, workers):
    return lax.ppermute(x, "worker", [(i, i ^ step) for i in range(workers)])


def split(me, pieces):
    workers, rows, lanes = pieces.shape
    order = sorted(range(workers), key=lambda d: -d)

    def kernel(me_ref, pieces_ref, *refs):
        high, (give, keep, buffer, sems) = refs[:workers], refs[workers:]
        copies = {}
        for d in order:
            copies[d] = pltpu.make_async_copy(
                pieces_ref.at[me_ref[0] ^ d], buffer.at[d], sems.at[d]
            )
            copies[d].start()
        for d in order:
            copies[d].wait()
            value = buffer[d]
            rounded = value.astype(jnp.bfloat16)
            high[d][...] = rounded
            low = (value - rounded.astype(jnp.float32)).astype(jnp.bfloat16)
            (give if d & 1 else keep)[d >> 1] = low

    piece = pltpu.VMEM((rows, lanes), jnp.bfloat16)
    half = pltpu.VMEM((workers // 2, rows, lanes), jnp.bfloat16)
    return pl.pallas_call(
        kernel,
        out_shape=(piece,) * workers + (half, half),
        in_specs=[
            pl.BlockSpec(memory_space=pltpu.SMEM),
            pl.BlockSpec(memory_space=pl.ANY),
        ],
        out_specs=(pl.BlockSpec(memory_space=pltpu.VMEM),) * (workers + 2),
        scratch_shapes=[
            pltpu.VMEM((workers, rows, lanes), jnp.float32),
            pltpu.SemaphoreType.DMA((workers,)),
        ],
        name="split",
    )(me, pieces)


def partial_scores(counts, blocks, devices, scale):
    workers = len(blocks)
    rows, lanes = blocks[0].shape
    pairs = [(a, b) for a in range(workers) for b in range(a + 1, workers)]
    chunk = 16

    def kernel(counts_ref, *refs):
        blocks_ref, out = refs[:workers], refs[workers]

        def step(r, sums):
            at = pl.ds(pl.multiple_of(r * chunk, chunk), chunk)
            rows_of = [ref[at, :].astype(jnp.float32) for ref in blocks_ref]
            new = []
            for (a, b), total in zip(pairs, sums):
                diff = rows_of[a] - rows_of[b]
                square = diff * diff
                new.append(total + square[:8] + square[8:])
            return tuple(new)

        zero = jnp.zeros((8, lanes), jnp.float32)
        sums = lax.fori_loop(0, rows // chunk, step, (zero,) * len(pairs))
        lane = lax.broadcasted_iota(jnp.int32, (1, lanes), 1)
        row = jnp.zeros((1, lanes), jnp.float32)
        own = [zero] * workers
        for (a, b), total in zip(pairs, sums):
            own[a] = own[a] + counts_ref[a, b] * total
            own[b] = own[b] + counts_ref[b, a] * total
        me = counts_ref[workers, 0].astype(jnp.int32)
        for a in range(workers):
            total = jnp.sum(jnp.sum(own[a], axis=0, keepdims=True), axis=1, keepdims=True)
            row = jnp.where(lane == me ^ a, total * scale, row)
        out[...] = jnp.broadcast_to(row[None], out.shape)

    return pl.pallas_call(
        kernel,
        out_shape=pltpu.VMEM((devices, 1, LANES), jnp.float32),
        in_specs=[pl.BlockSpec(memory_space=pltpu.SMEM)]
        + [pl.BlockSpec(memory_space=pltpu.VMEM)] * workers,
        out_specs=pl.BlockSpec(memory_space=pltpu.VMEM),
        name="scores",
    )(counts, *blocks)


def merge(place, blocks, lows):
    workers = len(blocks)

    def kernel(place_ref, *refs):
        high, low, out = refs[:workers], refs[workers:-1], refs[-1]
        for d in range(workers):

            @pl.when(place_ref[0] == d)
            def _(d=d):
                out[...] = high[d][...].astype(jnp.float32) + low[d >> 1][...].astype(jnp.float32)

    return pl.pallas_call(
        kernel,
        out_shape=jax.ShapeDtypeStruct(blocks[0].shape, jnp.float32),
        in_specs=[pl.BlockSpec(memory_space=pltpu.SMEM)]
        + [pl.BlockSpec(memory_space=pltpu.VMEM)] * (workers + len(lows)),
        out_specs=pl.BlockSpec(memory_space=pltpu.VMEM),
        name="merge",
    )(place, *blocks, *lows)


def layer(gradients, neighbours, winner):
    workers = lax.axis_size("worker")
    devices = workers * lax.axis_size("mp")
    me = lax.axis_index("worker")
    length = gradients.shape[1]
    rows = length // workers // LANES
    pieces = gradients.reshape(workers, rows, LANES)
    parts = split(me.reshape(1), pieces)
    high, give, keep = parts[:workers], parts[workers], parts[workers + 1]
    blocks = [high[0]]
    for d in range(1, workers):
        blocks.append(exchange(high[d], d, workers))
    blocks = [on_chip(block) for block in blocks]

    place = winner ^ me
    got = exchange(give, 1, workers)
    mine = jnp.where((place[0] & 1) == 0, keep, got)
    lows = [mine[0]]
    for j in range(1, workers // 2):
        lows.append(exchange(mine[j], 2 * j, workers))
    lows = [on_chip(low) for low in lows]

    index = jnp.arange(workers, dtype=jnp.int32) ^ me
    named = (neighbours[:, :, None] == index[None, None, :]).astype(jnp.float32).sum(axis=1)
    mine_rows = (index[:, None] == jnp.arange(workers, dtype=jnp.int32)[None, :]).astype(jnp.float32)
    counts = (mine_rows[:, :, None] * named[None]).sum(axis=1)
    counts = jnp.concatenate([counts, jnp.full((1, workers), me.astype(jnp.float32))], axis=0)
    scale = 1.0 / float(neighbours.shape[1] * length * lax.axis_size("mp"))
    partial_value = partial_scores(counts, blocks, devices, scale)
    everyone = lax.all_to_all(
        partial_value, ("worker", "mp"), split_axis=0, concat_axis=0, tiled=True
    )
    scores = jnp.sum(everyone, axis=0)[0, :workers]
    aggregate = merge(place, blocks, lows)
    return (scores, aggregate.reshape(-1))


def solution(mesh):
    in_specs = (P("worker", "mp"), P(), P())
    out_specs = (P(), P(("mp", "worker")))
    return jax.shard_map(layer, mesh=mesh, in_specs=in_specs, out_specs=out_specs, check_vma=False)
```

time: 108 us -> 45.8 us (0.42)
  blocking collectives: 39.8 us -> 0 us
  starting transfers between devices: 5.37 us -> 20.7 us
  other arithmetic: 14.3 us -> 0.35 us
  between operations: 14.7 us -> 1.35 us
  waiting for transfers between devices: 26.2 us -> 16.9 us
  Pallas kernels: 0 us -> 5.04 us
  local copies, waits for them, and re-layouts: 5.71 us -> 1.16 us
  matrix products: 1.2 us -> 0 us
    psum x1 -> x0, blocking collectives: 39.8 us -> none  [body(): gram_matrix = lax.psum(partial_value, ('worker', 'mp'))]
    ppermute x0 -> x11, starting transfers between devices: none -> 14.4 us  [exchange(): return lax.ppermute(x, 'worker', [(i, i ^ step) for i in range(workers)])]
    ppermute x0 -> x11, waiting for transfers between devices: none -> 10.4 us  [exchange(): return lax.ppermute(x, 'worker', [(i, i ^ step) for i in range(workers)])]
    all_to_all x1, waiting for transfers between devices: 16.4 us -> 6.47 us  [layer(): lax.all_to_all(partial_value, ('worker', 'mp'), split_axis=0, concat_axis...]
    psum x1 -> x0, waiting for transfers between devices: 9.12 us -> none  [from_root(): return lax.psum(block, axis)]
    unnamed x1 -> x0, other arithmetic: 7.03 us -> none
    select_n x1, other arithmetic: 6.5 us -> 0.06 us  [layer(): mine = jnp.where(place[0] & 1 == 0, keep, got)]
    pallas_call x0 -> x3, Pallas kernels: none -> 5.04 us  [the longest x1 2.66 us: partial_scores(): pl.pallas_call(kernel, out_shape=pltpu.VMEM((devices, 1, LANES), jnp.floa...]
  transfers between devices with their start and end apart: 2 -> 12, of which waited for: 2 -> 6; matrix products, arithmetic and copies ran while one was open for 3% -> 3% of each run, Pallas kernels for 0% -> 6%
where the time goes in v3:
time: 45.8 us; the launch traced here: 45.5 us
  starting transfers between devices  20.7 us (45%)
  waiting for transfers between devices  16.9 us (37%)
  Pallas kernels  5.04 us (11%)
  between operations  1.35 us (3%)
  local copies, waits for them, and re-layouts  1.16 us (3%)
    ppermute x11, starting transfers between devices, exchange(): return lax.ppermute(x, 'worker', [(i, i ^ step) for i in range(workers)])  14.4 us
    ppermute x11, waiting for transfers between devices, exchange(): return lax.ppermute(x, 'worker', [(i, i ^ step) for i in range(workers)])  10.4 us
    all_to_all x1, waiting for transfers between devices, layer(): lax.all_to_all(partial_value, ('worker', 'mp'), split_axis=0, concat_axis...  6.47 us
    all_to_all x1, starting transfers between devices, layer(): lax.all_to_all(partial_value, ('worker', 'mp'), split_axis=0, concat_axis...  6.36 us
    pallas_call x1, Pallas kernels, partial_scores(): pl.pallas_call(kernel, out_shape=pltpu.VMEM((devices, 1, LANES), jnp.floa...  2.66 us
    pallas_call x1, Pallas kernels, split(): pl.pallas_call(kernel, out_shape=(piece,) * workers + (half, half), in_sp...  1.61 us
  transfers between devices with their start and end apart: 12, of which 6 were waited for; matrix products, arithmetic and copies ran while one was open for 3% of the time, Pallas kernels for 6%

profile of v3, /device:TPU:0, one launch (start us, length us, event | category | flops | bytes accessed | tf_op | source)
XLA Modules:
  0.0 45.5 jit_solution(5391281424705435305)
XLA Ops:
  0.6 0.0 copy-start
  0.6 1.6 %split.1 = (bf16[512,128]{1,0:T(8,128)(2,1)S(1)}, bf16[512,128]{1,0:T(8,128)(2,1)S(1)}, bf16[512,128]{1,0:T(8,128)(2,1)S(1)}, bf16[512,128]{1,0:T(8,128)(2,1)S(1...) custom-call(s32[1]{0:T(128)} %bitcast.me_ref, ...), custom_call_target="tpu_custom_call" | custom-call | tf_op jit(solution)/shard_map/split/pallas_call | solution.py:41
  2.3 0.6 %collective-permute-start.7 = (bf16[4,512,128]{2,1,0:T(8,128)(2,1)S(1)}, bf16[4,512,128]{2,1,0:T(8,128)(2,1)S(1)}, u32[]{:S(2)}, u32[]{:S(2)}) collective-permute-start(bf16[4,512,128]{2,1,0:T(8,128)(2,1)S(1)} %get-tuple-element.21), channel_id=1, source_target_pairs={{0,4},{4,0},{8,12},{12,8},{16,20},{20,16},{24,28},{28,24},{1,5},{5... | collective-permute-start | bytes 1572872 | tf_op jit(solution)/shard_map/ppermute | solution.py:16
  2.8 0.1 collective-permute-start
  2.9 2.9 %collective-permute-start.1 = (bf16[512,128]{1,0:T(8,128)(2,1)S(1)}, bf16[512,128]{1,0:T(8,128)(2,1)S(1)}, u32[]{:S(2)}, u32[]{:S(2)}) collective-permute-start(bf16[512,128]{1,0:T(8,128)(2,1)S(1)} %get-tuple-element.14), channel_id=1, source_target_pairs={{0,8},{4,12},{8,0},{12,4},{16,24},{20,28},{24,16},{28,20},{1,9},{5... | collective-permute-start | bytes 393224 | tf_op jit(solution)/shard_map/ppermute | solution.py:16
  5.8 0.0 collective-permute-start.2
  5.8 1.5 %collective-permute-start.3 = (bf16[512,128]{1,0:T(8,128)(2,1)S(1)}, bf16[512,128]{1,0:T(8,128)(2,1)S(1)}, u32[]{:S(2)}, u32[]{:S(2)}) collective-permute-start(bf16[512,128]{1,0:T(8,128)(2,1)S(1)} %get-tuple-element.16), channel_id=1, source_target_pairs={{0,16},{4,20},{8,24},{12,28},{16,0},{20,4},{24,8},{28,12},{1,17},{... | collective-permute-start | bytes 393224 | tf_op jit(solution)/shard_map/ppermute | solution.py:16
  7.3 0.1 fusion
  7.4 0.0 collective-permute-done.refs_1_
  7.4 0.3 collective-permute-start.4
  7.7 2.5 %collective-permute-done.1.refs_2_ = bf16[512,128]{1,0:T(8,128)(2,1)S(1)} collective-permute-done((bf16[512,128]{1,0:T(8,128)(2,1)S(1)}, bf16[512,128]{1,0:T(8,128)(2,1)S(1)}, u32[]{:S(2)}, u32[]{:S(2)}) %collective-permute-start.1) | collective-permute-done | bytes 131104 | tf_op jit(solution)/shard_map/ppermute | solution.py:16
  10.2 3.0 %collective-permute-start.5 = (bf16[512,128]{1,0:T(8,128)(2,1)S(1)}, bf16[512,128]{1,0:T(8,128)(2,1)S(1)}, u32[]{:S(2)}, u32[]{:S(2)}) collective-permute-start(bf16[512,128]{1,0:T(8,128)(2,1)S(1)} %get-tuple-element.18), channel_id=1, source_target_pairs={{0,24},{4,28},{8,16},{12,20},{16,8},{20,12},{24,0},{28,4},{1,25},{... | collective-permute-start | bytes 393224 | tf_op jit(solution)/shard_map/ppermute | solution.py:16
  13.1 0.0 collective-permute-done.2.refs_3_
  13.1 2.5 %collective-permute-start.6 = (bf16[512,128]{1,0:T(8,128)(2,1)S(1)}, bf16[512,128]{1,0:T(8,128)(2,1)S(1)}, u32[]{:S(2)}, u32[]{:S(2)}) collective-permute-start(bf16[512,128]{1,0:T(8,128)(2,1)S(1)} %get-tuple-element.19), channel_id=1, source_target_pairs={{0,28},{4,24},{8,20},{12,16},{16,12},{20,8},{24,4},{28,0},{1,29},{... | collective-permute-start | bytes 393224 | tf_op jit(solution)/shard_map/ppermute | solution.py:16
  15.7 0.0 copy-done
  15.7 0.1 convert_reduce_fusion
  15.7 0.1 multiply_reduce_fusion
  15.8 0.6 %concatenate.3.counts_ref = f32[9,8]{1,0:T(8,128)} pad(f32[8,8]{1,0:T(8,128)S(1)} %multiply_reduce_fusion, f32[]{:T(128)S(6)} %convert_element_type.15), padding=0_1x0_0 | pad | bytes 548 | tf_op jit(solution)/shard_map/concatenate | solution.py:147
  16.4 0.0 collective-permute-done.3.refs_4_
  16.4 3.1 %collective-permute-done.4.refs_5_ = bf16[512,128]{1,0:T(8,128)(2,1)S(1)} collective-permute-done((bf16[512,128]{1,0:T(8,128)(2,1)S(1)}, bf16[512,128]{1,0:T(8,128)(2,1)S(1)}, u32[]{:S(2)}, u32[]{:S(2)}) %collective-permute-start.4) | collective-permute-done | bytes 131104 | tf_op jit(solution)/shard_map/ppermute | solution.py:16
  19.5 0.0 collective-permute-done.5.refs_6_
  19.5 0.0 collective-permute-done.6.refs_7_
  19.5 2.7 %scores.1 = f32[32,1,128]{2,1,0:T(1,128)} custom-call(f32[9,8]{1,0:T(8,128)} %concatenate.3.counts_ref, bf16[512,128]{1,0:T(8,128)(2,1)S(1)} %get-tuple-element.12.refs_0_, bf16[512,128]{1,0:T(8,128)(2,1)S(1)} %collective-permute-done.refs_1_, bf16[512,128]{1,0:T(8,128)(2,1)S(1)} %collective-permute-done.1.refs_2_, ...), custom_call_target="tpu_custom_call" | custom-call | tf_op jit(solution)/shard_map/scores/pallas_call | solution.py:90
  22.2 6.4 %all-to-all-start = ((f32[32,1,128]{2,1,0:T(1,128)}), f32[32,1,128]{2,1,0:T(1,128)S(1)}, u32[]{:S(2)}, u32[]{:S(2)}) async-start(f32[32,1,128]{2,1,0:T(1,128)} %scores.1), calls=%async_computation | async-start | bytes 32768 | tf_op jit(solution)/shard_map/all_to_all | solution.py:150
  29.2 6.5 %all-to-all-done = f32[32,1,128]{2,1,0:T(1,128)S(1)} async-done(((f32[32,1,128]{2,1,0:T(1,128)}), f32[32,1,128]{2,1,0:T(1,128)S(1)}, u32[]{:S(2)}, u32[]{:S(2)}) %all-to-all-start) | async-done | bytes 16416 | tf_op jit(solution)/shard_map/all_to_all | solution.py:150
  35.7 0.1 reduce_sum.31
  35.7 0.0 collective-permute-done.7
  35.7 0.1 broadcast_select_fusion
  35.8 0.6 %collective-permute-start.10 = (bf16[512,128]{1,0:T(8,128)(2,1)S(1)}, bf16[512,128]{1,0:T(8,128)(2,1)S(1)}, u32[]{:S(2)}, u32[]{:S(2)}) collective-permute-start(bf16[512,128]{1,0:T(8,128)(2,1)S(1)} %get-tuple-element.22), channel_id=1, source_target_pairs={{0,24},{4,28},{8,16},{12,20},{16,8},{20,12},{24,0},{28,4},{1,25},{... | collective-permute-start | bytes 393224 | tf_op jit(solution)/shard_map/ppermute | solution.py:16
  36.5 1.5 %collective-permute-start.8 = (bf16[512,128]{1,0:T(8,128)(2,1)S(1)}, bf16[512,128]{1,0:T(8,128)(2,1)S(1)}, u32[]{:S(2)}, u32[]{:S(2)}) collective-permute-start(bf16[512,128]{1,0:T(8,128)(2,1)S(1)} %get-tuple-element.24), channel_id=1, source_target_pairs={{0,8},{4,12},{8,0},{12,4},{16,24},{20,28},{24,16},{28,20},{1,9},{5... | collective-permute-start | bytes 393224 | tf_op jit(solution)/shard_map/ppermute | solution.py:16
  38.0 1.4 %collective-permute-start.9 = (bf16[512,128]{1,0:T(8,128)(2,1)S(1)}, bf16[512,128]{1,0:T(8,128)(2,1)S(1)}, u32[]{:S(2)}, u32[]{:S(2)}) collective-permute-start(bf16[512,128]{1,0:T(8,128)(2,1)S(1)} %get-tuple-element.23), channel_id=1, source_target_pairs={{0,16},{4,20},{8,24},{12,28},{16,0},{20,4},{24,8},{28,12},{1,17},{... | collective-permute-start | bytes 393224 | tf_op jit(solution)/shard_map/ppermute | solution.py:16
  39.4 0.5 %slice_bitcast_fusion.4 = f32[8]{0:T(128)} fusion(f32[1,128]{1,0:T(1,128)S(1)} %bitcast.17), kind=kLoop, calls=%fused_computation.9 | loop fusion | bytes 64 | tf_op jit(solution)/shard_map/squeeze | solution.py:153
  39.9 3.3 %collective-permute-done.10.refs_11_ = bf16[512,128]{1,0:T(8,128)(2,1)S(1)} collective-permute-done((bf16[512,128]{1,0:T(8,128)(2,1)S(1)}, bf16[512,128]{1,0:T(8,128)(2,1)S(1)}, u32[]{:S(2)}, u32[]{:S(2)}) %collective-permute-start.10) | collective-permute-done | bytes 131104 | tf_op jit(solution)/shard_map/ppermute | solution.py:16
  43.2 0.7 %collective-permute-done.8.refs_9_ = bf16[512,128]{1,0:T(8,128)(2,1)S(1)} collective-permute-done((bf16[512,128]{1,0:T(8,128)(2,1)S(1)}, bf16[512,128]{1,0:T(8,128)(2,1)S(1)}, u32[]{:S(2)}, u32[]{:S(2)}) %collective-permute-start.8) | collective-permute-done | bytes 131104 | tf_op jit(solution)/shard_map/ppermute | solution.py:16
  43.9 0.9 %collective-permute-done.9.refs_10_ = bf16[512,128]{1,0:T(8,128)(2,1)S(1)} collective-permute-done((bf16[512,128]{1,0:T(8,128)(2,1)S(1)}, bf16[512,128]{1,0:T(8,128)(2,1)S(1)}, u32[]{:S(2)}, u32[]{:S(2)}) %collective-permute-start.9) | collective-permute-done | bytes 131104 | tf_op jit(solution)/shard_map/ppermute | solution.py:16
  44.8 0.8 %merge.1 = f32[512,128]{1,0:T(8,128)} custom-call(s32[1]{0:T(128)S(6)} %xor.20.place_ref, bf16[512,128]{1,0:T(8,128)(2,1)S(1)} %get-tuple-element.12.refs_0_, bf16[512,128]{1,0:T(8,128)(2,1)S(1)} %collective-permute-done.refs_1_, bf16[512,128]{1,0:T(8,128)(2,1)S(1)} %collective-permute-done.1.refs_2_, bf16[512,128]{1,0:T(8,128)(2,1)S(1)} %collective-permute-done.2.refs_3_, ...), custom_call_target="tpu_custom_call" | custom-call | tf_op jit(solution)/shard_map/merge/pallas_call | solution.py:111
  (2 shorter events, 0.0 us)
Async XLA Ops:
  0.6 15.0 %copy-start = (s32[8,3]{0,1:T(4,128)S(1)}, s32[8,3]{0,1:T(4,128)}, u32[]{:S(2)}) copy-start(s32[8,3]{0,1:T(4,128)} %param.4) | copy-start | bytes 292
  2.3 33.5 %collective-permute-start.7 = (bf16[4,512,128]{2,1,0:T(8,128)(2,1)S(1)}, bf16[4,512,128]{2,1,0:T(8,128)(2,1)S(1)}, u32[]{:S(2)}, u32[]{:S(2)}) collective-permute-start(bf16[4,512,128]{2,1,0:T(8,128)(2,1)S(1)} %get-tuple-element.21), channel_id=1, source_target_pairs={{0,4},{4,0},{8,12},{12,8},{16,20},{20,16},{24,28},{28,24},{1,5},{5... | collective-permute-start | bytes 1572872 | tf_op jit(solution)/shard_map/ppermute | solution.py:16
  2.8 4.6 %collective-permute-start = (bf16[512,128]{1,0:T(8,128)(2,1)S(1)}, bf16[512,128]{1,0:T(8,128)(2,1)S(1)}, u32[]{:S(2)}, u32[]{:S(2)}) collective-permute-start(bf16[512,128]{1,0:T(8,128)(2,1)S(1)} %get-tuple-element.13), channel_id=1, source_target_pairs={{0,4},{4,0},{8,12},{12,8},{16,20},{20,16},{24,28},{28,24},{1,5},{5... | collective-permute-start | bytes 393224 | tf_op jit(solution)/shard_map/ppermute | solution.py:16
  2.9 7.3 %collective-permute-start.1 = (bf16[512,128]{1,0:T(8,128)(2,1)S(1)}, bf16[512,128]{1,0:T(8,128)(2,1)S(1)}, u32[]{:S(2)}, u32[]{:S(2)}) collective-permute-start(bf16[512,128]{1,0:T(8,128)(2,1)S(1)} %get-tuple-element.14), channel_id=1, source_target_pairs={{0,8},{4,12},{8,0},{12,4},{16,24},{20,28},{24,16},{28,20},{1,9},{5... | collective-permute-start | bytes 393224 | tf_op jit(solution)/shard_map/ppermute | solution.py:16
  5.8 7.3 %collective-permute-start.2 = (bf16[512,128]{1,0:T(8,128)(2,1)S(1)}, bf16[512,128]{1,0:T(8,128)(2,1)S(1)}, u32[]{:S(2)}, u32[]{:S(2)}) collective-permute-start(bf16[512,128]{1,0:T(8,128)(2,1)S(1)} %get-tuple-element.15), channel_id=1, source_target_pairs={{0,12},{4,8},{8,4},{12,0},{16,28},{20,24},{24,20},{28,16},{1,13},{... | collective-permute-start | bytes 393224 | tf_op jit(solution)/shard_map/ppermute | solution.py:16
  5.8 10.6 %collective-permute-start.3 = (bf16[512,128]{1,0:T(8,128)(2,1)S(1)}, bf16[512,128]{1,0:T(8,128)(2,1)S(1)}, u32[]{:S(2)}, u32[]{:S(2)}) collective-permute-start(bf16[512,128]{1,0:T(8,128)(2,1)S(1)} %get-tuple-element.16), channel_id=1, source_target_pairs={{0,16},{4,20},{8,24},{12,28},{16,0},{20,4},{24,8},{28,12},{1,17},{... | collective-permute-start | bytes 393224 | tf_op jit(solution)/shard_map/ppermute | solution.py:16
  7.4 12.1 %collective-permute-start.4 = (bf16[512,128]{1,0:T(8,128)(2,1)S(1)}, bf16[512,128]{1,0:T(8,128)(2,1)S(1)}, u32[]{:S(2)}, u32[]{:S(2)}) collective-permute-start(bf16[512,128]{1,0:T(8,128)(2,1)S(1)} %get-tuple-element.17), channel_id=1, source_target_pairs={{0,20},{4,16},{8,28},{12,24},{16,4},{20,0},{24,12},{28,8},{1,21},{... | collective-permute-start | bytes 393224 | tf_op jit(solution)/shard_map/ppermute | solution.py:16
  10.2 9.4 %collective-permute-start.5 = (bf16[512,128]{1,0:T(8,128)(2,1)S(1)}, bf16[512,128]{1,0:T(8,128)(2,1)S(1)}, u32[]{:S(2)}, u32[]{:S(2)}) collective-permute-start(bf16[512,128]{1,0:T(8,128)(2,1)S(1)} %get-tuple-element.18), channel_id=1, source_target_pairs={{0,24},{4,28},{8,16},{12,20},{16,8},{20,12},{24,0},{28,4},{1,25},{... | collective-permute-start | bytes 393224 | tf_op jit(solution)/shard_map/ppermute | solution.py:16
  13.1 6.4 %collective-permute-start.6 = (bf16[512,128]{1,0:T(8,128)(2,1)S(1)}, bf16[512,128]{1,0:T(8,128)(2,1)S(1)}, u32[]{:S(2)}, u32[]{:S(2)}) collective-permute-start(bf16[512,128]{1,0:T(8,128)(2,1)S(1)} %get-tuple-element.19), channel_id=1, source_target_pairs={{0,28},{4,24},{8,20},{12,16},{16,12},{20,8},{24,4},{28,0},{1,29},{... | collective-permute-start | bytes 393224 | tf_op jit(solution)/shard_map/ppermute | solution.py:16
  22.2 13.5 %all-to-all-start = ((f32[32,1,128]{2,1,0:T(1,128)}), f32[32,1,128]{2,1,0:T(1,128)S(1)}, u32[]{:S(2)}, u32[]{:S(2)}) async-start(f32[32,1,128]{2,1,0:T(1,128)} %scores.1), calls=%async_computation | async-start | bytes 32768 | tf_op jit(solution)/shard_map/all_to_all | solution.py:150
  35.8 7.3 %collective-permute-start.10 = (bf16[512,128]{1,0:T(8,128)(2,1)S(1)}, bf16[512,128]{1,0:T(8,128)(2,1)S(1)}, u32[]{:S(2)}, u32[]{:S(2)}) collective-permute-start(bf16[512,128]{1,0:T(8,128)(2,1)S(1)} %get-tuple-element.22), channel_id=1, source_target_pairs={{0,24},{4,28},{8,16},{12,20},{16,8},{20,12},{24,0},{28,4},{1,25},{... | collective-permute-start | bytes 393224 | tf_op jit(solution)/shard_map/ppermute | solution.py:16
  36.5 7.5 %collective-permute-start.8 = (bf16[512,128]{1,0:T(8,128)(2,1)S(1)}, bf16[512,128]{1,0:T(8,128)(2,1)S(1)}, u32[]{:S(2)}, u32[]{:S(2)}) collective-permute-start(bf16[512,128]{1,0:T(8,128)(2,1)S(1)} %get-tuple-element.24), channel_id=1, source_target_pairs={{0,8},{4,12},{8,0},{12,4},{16,24},{20,28},{24,16},{28,20},{1,9},{5... | collective-permute-start | bytes 393224 | tf_op jit(solution)/shard_map/ppermute | solution.py:16
  38.0 6.8 %collective-permute-start.9 = (bf16[512,128]{1,0:T(8,128)(2,1)S(1)}, bf16[512,128]{1,0:T(8,128)(2,1)S(1)}, u32[]{:S(2)}, u32[]{:S(2)}) collective-permute-start(bf16[512,128]{1,0:T(8,128)(2,1)S(1)} %get-tuple-element.23), channel_id=1, source_target_pairs={{0,16},{4,20},{8,24},{12,28},{16,0},{20,4},{24,8},{28,12},{1,17},{... | collective-permute-start | bytes 393224 | tf_op jit(solution)/shard_map/ppermute | solution.py:16

commit v4 on v3

--- a/solution.py
+++ b/solution.py
@@ -54,13 +54,13 @@
     )(me, pieces)
 
 
-def partial_scores(counts, blocks, devices, scale):
+def partial_scores(weights, blocks, devices):
     workers = len(blocks)
     rows, lanes = blocks[0].shape
     pairs = [(a, b) for a in range(workers) for b in range(a + 1, workers)]
     chunk = 16
 
-    def kernel(counts_ref, *refs):
+    def kernel(weights_ref, *refs):
         blocks_ref, out = refs[:workers], refs[workers]
 
         def step(r, sums):
@@ -75,26 +75,23 @@
 
         zero = jnp.zeros((8, lanes), jnp.float32)
         sums = lax.fori_loop(0, rows // chunk, step, (zero,) * len(pairs))
-        lane = lax.broadcasted_iota(jnp.int32, (1, lanes), 1)
-        row = jnp.zeros((1, lanes), jnp.float32)
         own = [zero] * workers
         for (a, b), total in zip(pairs, sums):
-            own[a] = own[a] + counts_ref[a, b] * total
-            own[b] = own[b] + counts_ref[b, a] * total
-        me = counts_ref[workers, 0].astype(jnp.int32)
+            own[a] = own[a] + weights_ref[a * workers + b][None] * total
+            own[b] = own[b] + weights_ref[b * workers + a][None] * total
+        row = jnp.zeros((1, lanes), jnp.float32)
         for a in range(workers):
             total = jnp.sum(jnp.sum(own[a], axis=0, keepdims=True), axis=1, keepdims=True)
-            row = jnp.where(lane == me ^ a, total * scale, row)
+            row = row + total * weights_ref[workers * workers + a][None]
         out[...] = jnp.broadcast_to(row[None], out.shape)
 
     return pl.pallas_call(
         kernel,
         out_shape=pltpu.VMEM((devices, 1, LANES), jnp.float32),
-        in_specs=[pl.BlockSpec(memory_space=pltpu.SMEM)]
-        + [pl.BlockSpec(memory_space=pltpu.VMEM)] * workers,
+        in_specs=[pl.BlockSpec(memory_space=pltpu.VMEM)] * (workers + 1),
         out_specs=pl.BlockSpec(memory_space=pltpu.VMEM),
         name="scores",
-    )(counts, *blocks)
+    )(weights, *blocks)
 
 
 def merge(place, blocks, lows):
@@ -140,13 +137,15 @@
         lows.append(exchange(mine[j], 2 * j, workers))
     lows = [on_chip(low) for low in lows]
 
+    scale = 1.0 / float(neighbours.shape[1] * length * lax.axis_size("mp"))
     index = jnp.arange(workers, dtype=jnp.int32) ^ me
     named = (neighbours[:, :, None] == index[None, None, :]).astype(jnp.float32).sum(axis=1)
-    mine_rows = (index[:, None] == jnp.arange(workers, dtype=jnp.int32)[None, :]).astype(jnp.float32)
-    counts = (mine_rows[:, :, None] * named[None]).sum(axis=1)
-    counts = jnp.concatenate([counts, jnp.full((1, workers), me.astype(jnp.float32))], axis=0)
-    scale = 1.0 / float(neighbours.shape[1] * length * lax.axis_size("mp"))
-    partial_value = partial_scores(counts, blocks, devices, scale)
+    is_row = (index[:, None] == jnp.arange(workers, dtype=jnp.int32)[None, :]).astype(jnp.float32)
+    counts = (is_row[:, :, None] * named[None]).sum(axis=1).reshape(-1, 1)
+    lane = jnp.arange(LANES, dtype=jnp.int32)[None, :]
+    places = jnp.where(lane == index[:, None], jnp.float32(scale), jnp.float32(0.0))
+    weights = jnp.concatenate([jnp.broadcast_to(counts, (workers * workers, LANES)), places])
+    partial_value = partial_scores(on_chip(weights), blocks, devices)
     everyone = lax.all_to_all(
         partial_value, ("worker", "mp"), split_axis=0, concat_axis=0, tiled=True
     )

time: 45.8 us -> 44.9 us (0.980)
  Pallas kernels: 5.04 us -> 4.22 us
  local copies, waits for them, and re-layouts: 1.16 us -> 0.64 us
    pallas_call x1, Pallas kernels: 2.66 us -> 1.85 us  [partial_scores(): pl.pallas_call(kernel, out_shape=pltpu.VMEM((devices, 1, LANES), jnp.floa...]
    concatenate x1, local copies, waits for them, and re-layouts: 0.6 us -> 0.01 us  [layer(): jnp.concatenate([jnp.broadcast_to(counts, (workers * workers, LANES)), pl...]
  transfers between devices with their start and end apart: 12 -> 12, of which waited for: 6 -> 6; matrix products, arithmetic and copies ran while one was open for 3% -> 2% of each run, Pallas kernels for 6% -> 4%
where the time goes in v4:
time: 44.9 us; the launch traced here: 44.7 us
  starting transfers between devices  20.7 us (46%)
  waiting for transfers between devices  17.3 us (39%)
  Pallas kernels  4.22 us (9%)
  between operations  1.35 us (3%)
  local copies, waits for them, and re-layouts  0.64 us (1%)
  other arithmetic  0.49 us (1%)
    ppermute x11, starting transfers between devices, exchange(): return lax.ppermute(x, 'worker', [(i, i ^ step) for i in range(workers)])  14.4 us
    ppermute x11, waiting for transfers between devices, exchange(): return lax.ppermute(x, 'worker', [(i, i ^ step) for i in range(workers)])  10.8 us
    all_to_all x1, waiting for transfers between devices, layer(): lax.all_to_all(partial_value, ('worker', 'mp'), split_axis=0, concat_axis...  6.47 us
    all_to_all x1, starting transfers between devices, layer(): lax.all_to_all(partial_value, ('worker', 'mp'), split_axis=0, concat_axis...  6.36 us
    pallas_call x1, Pallas kernels, partial_scores(): pl.pallas_call(kernel, out_shape=pltpu.VMEM((devices, 1, LANES), jnp.floa...  1.85 us
    pallas_call x1, Pallas kernels, split(): pl.pallas_call(kernel, out_shape=(piece,) * workers + (half, half), in_sp...  1.61 us
  transfers between devices with their start and end apart: 12, of which 6 were waited for; matrix products, arithmetic and copies ran while one was open for 2% of the time, Pallas kernels for 4%

profile of v4, /device:TPU:0, one launch (start us, length us, event | category | flops | bytes accessed | tf_op | source)
XLA Modules:
  0.0 44.7 jit_solution(11777073658383065228)
XLA Ops:
  0.6 0.0 copy-start
  0.6 1.6 %split.1 = (bf16[512,128]{1,0:T(8,128)(2,1)S(1)}, bf16[512,128]{1,0:T(8,128)(2,1)S(1)}, bf16[512,128]{1,0:T(8,128)(2,1)S(1)}, bf16[512,128]{1,0:T(8,128)(2,1)S(1...) custom-call(s32[1]{0:T(128)} %bitcast.me_ref, ...), custom_call_target="tpu_custom_call" | custom-call | tf_op jit(solution)/shard_map/split/pallas_call | solution.py:41
  2.3 0.6 %collective-permute-start.7 = (bf16[4,512,128]{2,1,0:T(8,128)(2,1)S(1)}, bf16[4,512,128]{2,1,0:T(8,128)(2,1)S(1)}, u32[]{:S(2)}, u32[]{:S(2)}) collective-permute-start(bf16[4,512,128]{2,1,0:T(8,128)(2,1)S(1)} %get-tuple-element.21), channel_id=1, source_target_pairs={{0,4},{4,0},{8,12},{12,8},{16,20},{20,16},{24,28},{28,24},{1,5},{5... | collective-permute-start | bytes 1572872 | tf_op jit(solution)/shard_map/ppermute | solution.py:16
  2.8 0.1 collective-permute-start
  2.9 2.9 %collective-permute-start.1 = (bf16[512,128]{1,0:T(8,128)(2,1)S(1)}, bf16[512,128]{1,0:T(8,128)(2,1)S(1)}, u32[]{:S(2)}, u32[]{:S(2)}) collective-permute-start(bf16[512,128]{1,0:T(8,128)(2,1)S(1)} %get-tuple-element.14), channel_id=1, source_target_pairs={{0,8},{4,12},{8,0},{12,4},{16,24},{20,28},{24,16},{28,20},{1,9},{5... | collective-permute-start | bytes 393224 | tf_op jit(solution)/shard_map/ppermute | solution.py:16
  5.8 0.0 collective-permute-start.2
  5.8 1.5 %collective-permute-start.3 = (bf16[512,128]{1,0:T(8,128)(2,1)S(1)}, bf16[512,128]{1,0:T(8,128)(2,1)S(1)}, u32[]{:S(2)}, u32[]{:S(2)}) collective-permute-start(bf16[512,128]{1,0:T(8,128)(2,1)S(1)} %get-tuple-element.16), channel_id=1, source_target_pairs={{0,16},{4,20},{8,24},{12,28},{16,0},{20,4},{24,8},{28,12},{1,17},{... | collective-permute-start | bytes 393224 | tf_op jit(solution)/shard_map/ppermute | solution.py:16
  7.3 0.1 fusion
  7.4 0.0 copy-done
  7.4 0.1 convert_reduce_fusion
  7.5 0.1 multiply_reduce_fusion
  7.6 0.1 reshape.54
  7.7 0.1 fusion.1
  7.7 0.0 collective-permute-done.refs_1_
  7.7 0.3 collective-permute-start.4
  8.0 2.1 %collective-permute-done.1.refs_2_ = bf16[512,128]{1,0:T(8,128)(2,1)S(1)} collective-permute-done((bf16[512,128]{1,0:T(8,128)(2,1)S(1)}, bf16[512,128]{1,0:T(8,128)(2,1)S(1)}, u32[]{:S(2)}, u32[]{:S(2)}) %collective-permute-start.1) | collective-permute-done | bytes 131104 | tf_op jit(solution)/shard_map/ppermute | solution.py:16
  10.2 3.0 %collective-permute-start.5 = (bf16[512,128]{1,0:T(8,128)(2,1)S(1)}, bf16[512,128]{1,0:T(8,128)(2,1)S(1)}, u32[]{:S(2)}, u32[]{:S(2)}) collective-permute-start(bf16[512,128]{1,0:T(8,128)(2,1)S(1)} %get-tuple-element.18), channel_id=1, source_target_pairs={{0,24},{4,28},{8,16},{12,20},{16,8},{20,12},{24,0},{28,4},{1,25},{... | collective-permute-start | bytes 393224 | tf_op jit(solution)/shard_map/ppermute | solution.py:16
  13.1 0.0 collective-permute-done.2.refs_3_
  13.1 2.5 %collective-permute-start.6 = (bf16[512,128]{1,0:T(8,128)(2,1)S(1)}, bf16[512,128]{1,0:T(8,128)(2,1)S(1)}, u32[]{:S(2)}, u32[]{:S(2)}) collective-permute-start(bf16[512,128]{1,0:T(8,128)(2,1)S(1)} %get-tuple-element.19), channel_id=1, source_target_pairs={{0,28},{4,24},{8,20},{12,16},{16,12},{20,8},{24,4},{28,0},{1,29},{... | collective-permute-start | bytes 393224 | tf_op jit(solution)/shard_map/ppermute | solution.py:16
  15.7 0.1 pad_maximum_fusion.weights_ref
  15.7 0.0 collective-permute-done.3.refs_4_
  15.7 3.8 %collective-permute-done.4.refs_5_ = bf16[512,128]{1,0:T(8,128)(2,1)S(1)} collective-permute-done((bf16[512,128]{1,0:T(8,128)(2,1)S(1)}, bf16[512,128]{1,0:T(8,128)(2,1)S(1)}, u32[]{:S(2)}, u32[]{:S(2)}) %collective-permute-start.4) | collective-permute-done | bytes 131104 | tf_op jit(solution)/shard_map/ppermute | solution.py:16
  19.5 0.0 collective-permute-done.5.refs_6_
  19.5 0.0 collective-permute-done.6.refs_7_
  19.5 1.8 %scores.1 = f32[32,1,128]{2,1,0:T(1,128)} custom-call(f32[72,128]{1,0:T(8,128)S(1)} %pad_maximum_fusion.weights_ref, bf16[512,128]{1,0:T(8,128)(2,1)S(1)} %get-tuple-element.12.refs_0_, bf16[512,128]{1,0:T(8,128)(2,1)S(1)} %collective-permute-done.refs_1_, bf16[512,128]{1,0:T(8,128)(2,1)S(1)} %collective-permute-done.1.refs_2_, ...), custom_call_target="tpu_custom_call" | custom-call | tf_op jit(solution)/shard_map/scores/pallas_call | solution.py:88
  21.4 6.4 %all-to-all-start = ((f32[32,1,128]{2,1,0:T(1,128)}), f32[32,1,128]{2,1,0:T(1,128)S(1)}, u32[]{:S(2)}, u32[]{:S(2)}) async-start(f32[32,1,128]{2,1,0:T(1,128)} %scores.1), calls=%async_computation | async-start | bytes 32768 | tf_op jit(solution)/shard_map/all_to_all | solution.py:149
  28.4 6.5 %all-to-all-done = f32[32,1,128]{2,1,0:T(1,128)S(1)} async-done(((f32[32,1,128]{2,1,0:T(1,128)}), f32[32,1,128]{2,1,0:T(1,128)S(1)}, u32[]{:S(2)}, u32[]{:S(2)}) %all-to-all-start) | async-done | bytes 16416 | tf_op jit(solution)/shard_map/all_to_all | solution.py:149
  34.9 0.1 reduce_sum.31
  34.9 0.0 collective-permute-done.7
  34.9 0.1 broadcast_select_fusion
  35.0 0.6 %collective-permute-start.10 = (bf16[512,128]{1,0:T(8,128)(2,1)S(1)}, bf16[512,128]{1,0:T(8,128)(2,1)S(1)}, u32[]{:S(2)}, u32[]{:S(2)}) collective-permute-start(bf16[512,128]{1,0:T(8,128)(2,1)S(1)} %get-tuple-element.22), channel_id=1, source_target_pairs={{0,24},{4,28},{8,16},{12,20},{16,8},{20,12},{24,0},{28,4},{1,25},{... | collective-permute-start | bytes 393224 | tf_op jit(solution)/shard_map/ppermute | solution.py:16
  35.6 1.5 %collective-permute-start.8 = (bf16[512,128]{1,0:T(8,128)(2,1)S(1)}, bf16[512,128]{1,0:T(8,128)(2,1)S(1)}, u32[]{:S(2)}, u32[]{:S(2)}) collective-permute-start(bf16[512,128]{1,0:T(8,128)(2,1)S(1)} %get-tuple-element.24), channel_id=1, source_target_pairs={{0,8},{4,12},{8,0},{12,4},{16,24},{20,28},{24,16},{28,20},{1,9},{5... | collective-permute-start | bytes 393224 | tf_op jit(solution)/shard_map/ppermute | solution.py:16
  37.1 1.4 %collective-permute-start.9 = (bf16[512,128]{1,0:T(8,128)(2,1)S(1)}, bf16[512,128]{1,0:T(8,128)(2,1)S(1)}, u32[]{:S(2)}, u32[]{:S(2)}) collective-permute-start(bf16[512,128]{1,0:T(8,128)(2,1)S(1)} %get-tuple-element.23), channel_id=1, source_target_pairs={{0,16},{4,20},{8,24},{12,28},{16,0},{20,4},{24,8},{28,12},{1,17},{... | collective-permute-start | bytes 393224 | tf_op jit(solution)/shard_map/ppermute | solution.py:16
  38.6 0.5 %slice_bitcast_fusion.4 = f32[8]{0:T(128)} fusion(f32[1,128]{1,0:T(1,128)S(1)} %bitcast.17), kind=kLoop, calls=%fused_computation.12 | loop fusion | bytes 64 | tf_op jit(solution)/shard_map/squeeze | solution.py:152
  39.1 3.3 %collective-permute-done.10.refs_11_ = bf16[512,128]{1,0:T(8,128)(2,1)S(1)} collective-permute-done((bf16[512,128]{1,0:T(8,128)(2,1)S(1)}, bf16[512,128]{1,0:T(8,128)(2,1)S(1)}, u32[]{:S(2)}, u32[]{:S(2)}) %collective-permute-start.10) | collective-permute-done | bytes 131104 | tf_op jit(solution)/shard_map/ppermute | solution.py:16
  42.4 0.7 %collective-permute-done.8.refs_9_ = bf16[512,128]{1,0:T(8,128)(2,1)S(1)} collective-permute-done((bf16[512,128]{1,0:T(8,128)(2,1)S(1)}, bf16[512,128]{1,0:T(8,128)(2,1)S(1)}, u32[]{:S(2)}, u32[]{:S(2)}) %collective-permute-start.8) | collective-permute-done | bytes 131104 | tf_op jit(solution)/shard_map/ppermute | solution.py:16
  43.1 0.9 %collective-permute-done.9.refs_10_ = bf16[512,128]{1,0:T(8,128)(2,1)S(1)} collective-permute-done((bf16[512,128]{1,0:T(8,128)(2,1)S(1)}, bf16[512,128]{1,0:T(8,128)(2,1)S(1)}, u32[]{:S(2)}, u32[]{:S(2)}) %collective-permute-start.9) | collective-permute-done | bytes 131104 | tf_op jit(solution)/shard_map/ppermute | solution.py:16
  44.0 0.8 %merge.1 = f32[512,128]{1,0:T(8,128)} custom-call(s32[1]{0:T(128)S(6)} %xor.20.place_ref, bf16[512,128]{1,0:T(8,128)(2,1)S(1)} %get-tuple-element.12.refs_0_, bf16[512,128]{1,0:T(8,128)(2,1)S(1)} %collective-permute-done.refs_1_, bf16[512,128]{1,0:T(8,128)(2,1)S(1)} %collective-permute-done.1.refs_2_, bf16[512,128]{1,0:T(8,128)(2,1)S(1)} %collective-permute-done.2.refs_3_, ...), custom_call_target="tpu_custom_call" | custom-call | tf_op jit(solution)/shard_map/merge/pallas_call | solution.py:108
  (3 shorter events, 0.0 us)
Async XLA Ops:
  0.6 6.8 %copy-start = (s32[8,3]{0,1:T(4,128)S(1)}, s32[8,3]{0,1:T(4,128)}, u32[]{:S(2)}) copy-start(s32[8,3]{0,1:T(4,128)} %param.4) | copy-start | bytes 292
  2.3 32.6 %collective-permute-start.7 = (bf16[4,512,128]{2,1,0:T(8,128)(2,1)S(1)}, bf16[4,512,128]{2,1,0:T(8,128)(2,1)S(1)}, u32[]{:S(2)}, u32[]{:S(2)}) collective-permute-start(bf16[4,512,128]{2,1,0:T(8,128)(2,1)S(1)} %get-tuple-element.21), channel_id=1, source_target_pairs={{0,4},{4,0},{8,12},{12,8},{16,20},{20,16},{24,28},{28,24},{1,5},{5... | collective-permute-start | bytes 1572872 | tf_op jit(solution)/shard_map/ppermute | solution.py:16
  2.8 4.9 %collective-permute-start = (bf16[512,128]{1,0:T(8,128)(2,1)S(1)}, bf16[512,128]{1,0:T(8,128)(2,1)S(1)}, u32[]{:S(2)}, u32[]{:S(2)}) collective-permute-start(bf16[512,128]{1,0:T(8,128)(2,1)S(1)} %get-tuple-element.13), channel_id=1, source_target_pairs={{0,4},{4,0},{8,12},{12,8},{16,20},{20,16},{24,28},{28,24},{1,5},{5... | collective-permute-start | bytes 393224 | tf_op jit(solution)/shard_map/ppermute | solution.py:16
  2.9 7.3 %collective-permute-start.1 = (bf16[512,128]{1,0:T(8,128)(2,1)S(1)}, bf16[512,128]{1,0:T(8,128)(2,1)S(1)}, u32[]{:S(2)}, u32[]{:S(2)}) collective-permute-start(bf16[512,128]{1,0:T(8,128)(2,1)S(1)} %get-tuple-element.14), channel_id=1, source_target_pairs={{0,8},{4,12},{8,0},{12,4},{16,24},{20,28},{24,16},{28,20},{1,9},{5... | collective-permute-start | bytes 393224 | tf_op jit(solution)/shard_map/ppermute | solution.py:16
  5.8 7.3 %collective-permute-start.2 = (bf16[512,128]{1,0:T(8,128)(2,1)S(1)}, bf16[512,128]{1,0:T(8,128)(2,1)S(1)}, u32[]{:S(2)}, u32[]{:S(2)}) collective-permute-start(bf16[512,128]{1,0:T(8,128)(2,1)S(1)} %get-tuple-element.15), channel_id=1, source_target_pairs={{0,12},{4,8},{8,4},{12,0},{16,28},{20,24},{24,20},{28,16},{1,13},{... | collective-permute-start | bytes 393224 | tf_op jit(solution)/shard_map/ppermute | solution.py:16
  5.8 9.9 %collective-permute-start.3 = (bf16[512,128]{1,0:T(8,128)(2,1)S(1)}, bf16[512,128]{1,0:T(8,128)(2,1)S(1)}, u32[]{:S(2)}, u32[]{:S(2)}) collective-permute-start(bf16[512,128]{1,0:T(8,128)(2,1)S(1)} %get-tuple-element.16), channel_id=1, source_target_pairs={{0,16},{4,20},{8,24},{12,28},{16,0},{20,4},{24,8},{28,12},{1,17},{... | collective-permute-start | bytes 393224 | tf_op jit(solution)/shard_map/ppermute | solution.py:16
  7.7 11.8 %collective-permute-start.4 = (bf16[512,128]{1,0:T(8,128)(2,1)S(1)}, bf16[512,128]{1,0:T(8,128)(2,1)S(1)}, u32[]{:S(2)}, u32[]{:S(2)}) collective-permute-start(bf16[512,128]{1,0:T(8,128)(2,1)S(1)} %get-tuple-element.17), channel_id=1, source_target_pairs={{0,20},{4,16},{8,28},{12,24},{16,4},{20,0},{24,12},{28,8},{1,21},{... | collective-permute-start | bytes 393224 | tf_op jit(solution)/shard_map/ppermute | solution.py:16
  10.2 9.4 %collective-permute-start.5 = (bf16[512,128]{1,0:T(8,128)(2,1)S(1)}, bf16[512,128]{1,0:T(8,128)(2,1)S(1)}, u32[]{:S(2)}, u32[]{:S(2)}) collective-permute-start(bf16[512,128]{1,0:T(8,128)(2,1)S(1)} %get-tuple-element.18), channel_id=1, source_target_pairs={{0,24},{4,28},{8,16},{12,20},{16,8},{20,12},{24,0},{28,4},{1,25},{... | collective-permute-start | bytes 393224 | tf_op jit(solution)/shard_map/ppermute | solution.py:16
  13.1 6.4 %collective-permute-start.6 = (bf16[512,128]{1,0:T(8,128)(2,1)S(1)}, bf16[512,128]{1,0:T(8,128)(2,1)S(1)}, u32[]{:S(2)}, u32[]{:S(2)}) collective-permute-start(bf16[512,128]{1,0:T(8,128)(2,1)S(1)} %get-tuple-element.19), channel_id=1, source_target_pairs={{0,28},{4,24},{8,20},{12,16},{16,12},{20,8},{24,4},{28,0},{1,29},{... | collective-permute-start | bytes 393224 | tf_op jit(solution)/shard_map/ppermute | solution.py:16
  21.4 13.5 %all-to-all-start = ((f32[32,1,128]{2,1,0:T(1,128)}), f32[32,1,128]{2,1,0:T(1,128)S(1)}, u32[]{:S(2)}, u32[]{:S(2)}) async-start(f32[32,1,128]{2,1,0:T(1,128)} %scores.1), calls=%async_computation | async-start | bytes 32768 | tf_op jit(solution)/shard_map/all_to_all | solution.py:149
  35.0 7.3 %collective-permute-start.10 = (bf16[512,128]{1,0:T(8,128)(2,1)S(1)}, bf16[512,128]{1,0:T(8,128)(2,1)S(1)}, u32[]{:S(2)}, u32[]{:S(2)}) collective-permute-start(bf16[512,128]{1,0:T(8,128)(2,1)S(1)} %get-tuple-element.22), channel_id=1, source_target_pairs={{0,24},{4,28},{8,16},{12,20},{16,8},{20,12},{24,0},{28,4},{1,25},{... | collective-permute-start | bytes 393224 | tf_op jit(solution)/shard_map/ppermute | solution.py:16
  35.6 7.5 %collective-permute-start.8 = (bf16[512,128]{1,0:T(8,128)(2,1)S(1)}, bf16[512,128]{1,0:T(8,128)(2,1)S(1)}, u32[]{:S(2)}, u32[]{:S(2)}) collective-permute-start(bf16[512,128]{1,0:T(8,128)(2,1)S(1)} %get-tuple-element.24), channel_id=1, source_target_pairs={{0,8},{4,12},{8,0},{12,4},{16,24},{20,28},{24,16},{28,20},{1,9},{5... | collective-permute-start | bytes 393224 | tf_op jit(solution)/shard_map/ppermute | solution.py:16
  37.1 6.8 %collective-permute-start.9 = (bf16[512,128]{1,0:T(8,128)(2,1)S(1)}, bf16[512,128]{1,0:T(8,128)(2,1)S(1)}, u32[]{:S(2)}, u32[]{:S(2)}) collective-permute-start(bf16[512,128]{1,0:T(8,128)(2,1)S(1)} %get-tuple-element.23), channel_id=1, source_target_pairs={{0,16},{4,20},{8,24},{12,28},{16,0},{20,4},{24,8},{28,12},{1,17},{... | collective-permute-start | bytes 393224 | tf_op jit(solution)/shard_map/ppermute | solution.py:16

commit v5 on v4

--- a/solution.py
+++ b/solution.py
@@ -16,41 +16,44 @@
     return lax.ppermute(x, "worker", [(i, i ^ step) for i in range(workers)])
 
 
-def split(me, pieces):
+def split(me, pieces, wanted, remainder):
     workers, rows, lanes = pieces.shape
-    order = sorted(range(workers), key=lambda d: -d)
+    order = sorted(range(workers) if remainder else wanted, key=lambda d: (d not in wanted, -d))
 
     def kernel(me_ref, pieces_ref, *refs):
-        high, (give, keep, buffer, sems) = refs[:workers], refs[workers:]
+        high = dict(zip(wanted, refs))
+        low_refs, (buffer, sems) = refs[len(wanted):-2], refs[-2:]
         copies = {}
-        for d in order:
+        for n, d in enumerate(order):
             copies[d] = pltpu.make_async_copy(
-                pieces_ref.at[me_ref[0] ^ d], buffer.at[d], sems.at[d]
+                pieces_ref.at[me_ref[0] ^ d], buffer.at[n], sems.at[n]
             )
             copies[d].start()
-        for d in order:
+        for n, d in enumerate(order):
             copies[d].wait()
-            value = buffer[d]
+            value = buffer[n]
             rounded = value.astype(jnp.bfloat16)
-            high[d][...] = rounded
-            low = (value - rounded.astype(jnp.float32)).astype(jnp.bfloat16)
-            (give if d & 1 else keep)[d >> 1] = low
+            if d in wanted:
+                high[d][...] = rounded
+            if remainder:
+                low = (value - rounded.astype(jnp.float32)).astype(jnp.bfloat16)
+                low_refs[d & 1][d >> 1] = low
 
     piece = pltpu.VMEM((rows, lanes), jnp.bfloat16)
     half = pltpu.VMEM((workers // 2, rows, lanes), jnp.bfloat16)
+    out_shape = (piece,) * len(wanted) + ((half, half) if remainder else ())
     return pl.pallas_call(
         kernel,
-        out_shape=(piece,) * workers + (half, half),
+        out_shape=out_shape,
         in_specs=[
             pl.BlockSpec(memory_space=pltpu.SMEM),
             pl.BlockSpec(memory_space=pl.ANY),
         ],
-        out_specs=(pl.BlockSpec(memory_space=pltpu.VMEM),) * (workers + 2),
+        out_specs=(pl.BlockSpec(memory_space=pltpu.VMEM),) * len(out_shape),
         scratch_shapes=[
-            pltpu.VMEM((workers, rows, lanes), jnp.float32),
-            pltpu.SemaphoreType.DMA((workers,)),
+            pltpu.VMEM((len(order), rows, lanes), jnp.float32),
+            pltpu.SemaphoreType.DMA((len(order),)),
         ],
-        name="split",
     )(me, pieces)
 
 
@@ -74,7 +77,7 @@
             return tuple(new)
 
         zero = jnp.zeros((8, lanes), jnp.float32)
-        sums = lax.fori_loop(0, rows // chunk, step, (zero,) * len(pairs))
+        sums = lax.fori_loop(0, rows // chunk, step, (zero,) * len(pairs), unroll=2)
         own = [zero] * workers
         for (a, b), total in zip(pairs, sums):
             own[a] = own[a] + weights_ref[a * workers + b][None] * total
@@ -122,8 +125,11 @@
     length = gradients.shape[1]
     rows = length // workers // LANES
     pieces = gradients.reshape(workers, rows, LANES)
-    parts = split(me.reshape(1), pieces)
-    high, give, keep = parts[:workers], parts[workers], parts[workers + 1]
+    first = list(range(2, workers, 2))
+    others = [d for d in range(workers) if d not in first]
+    high = dict(zip(first, split(me.reshape(1), pieces, first, False)))
+    *parts, keep, give = split(me.reshape(1), pieces, others, True)
+    high.update(zip(others, parts))
     blocks = [high[0]]
     for d in range(1, workers):
         blocks.append(exchange(high[d], d, workers))

time: 44.9 us -> 45.2 us (level)
  starting transfers between devices: 20.7 us -> 16.2 us
  waiting for transfers between devices: 17.3 us -> 21.1 us
  Pallas kernels: 4.22 us -> 5.19 us
    ppermute x11, waiting for transfers between devices: 10.8 us -> 14.7 us  [exchange(): return lax.ppermute(x, 'worker', [(i, i ^ step) for i in range(workers)])]
    ppermute x11, starting transfers between devices: 14.4 us -> 11.5 us  [exchange(): return lax.ppermute(x, 'worker', [(i, i ^ step) for i in range(workers)])]
    all_to_all x1, starting transfers between devices: 6.36 us -> 4.67 us  [layer(): lax.all_to_all(partial_value, ('worker', 'mp'), split_axis=0, concat_axis...]
    pallas_call x1 -> x2, Pallas kernels: 1.61 us -> 2.76 us  [split(): pl.pallas_call(kernel, out_shape=out_shape, in_specs=[pl.BlockSpec(memory...]
  transfers between devices with their start and end apart: 12 -> 12, of which waited for: 6 -> 8; matrix products, arithmetic and copies ran while one was open for 2% -> 2% of each run, Pallas kernels for 4% -> 6%
where the time goes in v5:
time: 45.2 us; the launch traced here: 45 us
  waiting for transfers between devices  21.1 us (47%)
  starting transfers between devices  16.2 us (36%)
  Pallas kernels  5.19 us (11%)
  between operations  1.36 us (3%)
  local copies, waits for them, and re-layouts  0.64 us (1%)
  other arithmetic  0.5 us (1%)
    ppermute x11, waiting for transfers between devices, exchange(): return lax.ppermute(x, 'worker', [(i, i ^ step) for i in range(workers)])  14.7 us
    ppermute x11, starting transfers between devices, exchange(): return lax.ppermute(x, 'worker', [(i, i ^ step) for i in range(workers)])  11.5 us
    all_to_all x1, waiting for transfers between devices, layer(): lax.all_to_all(partial_value, ('worker', 'mp'), split_axis=0, concat_axis...  6.47 us
    all_to_all x1, starting transfers between devices, layer(): lax.all_to_all(partial_value, ('worker', 'mp'), split_axis=0, concat_axis...  4.67 us
    pallas_call x2, Pallas kernels, split(): pl.pallas_call(kernel, out_shape=out_shape, in_specs=[pl.BlockSpec(memory...  2.76 us
    pallas_call x1, Pallas kernels, partial_scores(): pl.pallas_call(kernel, out_shape=pltpu.VMEM((devices, 1, LANES), jnp.floa...  1.66 us
  transfers between devices with their start and end apart: 12, of which 8 were waited for; matrix products, arithmetic and copies ran while one was open for 2% of the time, Pallas kernels for 6%

profile of v5, /device:TPU:0, one launch (start us, length us, event | category | flops | bytes accessed | tf_op | source)
XLA Modules:
  0.0 45.0 jit_solution(11563475679266531477)
XLA Ops:
  0.6 0.0 copy-start
  0.6 1.6 %shard_map.50 = (bf16[512,128]{1,0:T(8,128)(2,1)S(1)}, bf16[512,128]{1,0:T(8,128)(2,1)S(1)}, bf16[512,128]{1,0:T(8,128)(2,1)S(1)}, bf16[512,128]{1,0:T(8,128)(2,...) custom-call(s32[1]{0:T(128)} %bitcast.me_ref, ...), custom_call_target="tpu_custom_call" | custom-call | tf_op jit(solution)/shard_map/pallas_call | solution.py:45
  2.3 0.6 %collective-permute-start.7 = (bf16[4,512,128]{2,1,0:T(8,128)(2,1)S(1)}, bf16[4,512,128]{2,1,0:T(8,128)(2,1)}, u32[]{:S(2)}, u32[]{:S(2)}) collective-permute-start(bf16[4,512,128]{2,1,0:T(8,128)(2,1)S(1)} %get-tuple-element.21), channel_id=1, source_target_pairs={{0,4},{4,0},{8,12},{12,8},{16,20},{20,16},{24,28},{28,24},{1,5},{5... | collective-permute-start | bytes 1572872 | tf_op jit(solution)/shard_map/ppermute | solution.py:16
  2.8 0.1 collective-permute-start
  2.9 2.6 %collective-permute-start.2 = (bf16[512,128]{1,0:T(8,128)(2,1)S(1)}, bf16[512,128]{1,0:T(8,128)(2,1)S(1)}, u32[]{:S(2)}, u32[]{:S(2)}) collective-permute-start(bf16[512,128]{1,0:T(8,128)(2,1)S(1)} %get-tuple-element.15), channel_id=1, source_target_pairs={{0,12},{4,8},{8,4},{12,0},{16,28},{20,24},{24,20},{28,16},{1,13},{... | collective-permute-start | bytes 393224 | tf_op jit(solution)/shard_map/ppermute | solution.py:16
  5.5 1.6 %collective-permute-start.4 = (bf16[512,128]{1,0:T(8,128)(2,1)S(1)}, bf16[512,128]{1,0:T(8,128)(2,1)S(1)}, u32[]{:S(2)}, u32[]{:S(2)}) collective-permute-start(bf16[512,128]{1,0:T(8,128)(2,1)S(1)} %get-tuple-element.17), channel_id=1, source_target_pairs={{0,20},{4,16},{8,28},{12,24},{16,4},{20,0},{24,12},{28,8},{1,21},{... | collective-permute-start | bytes 393224 | tf_op jit(solution)/shard_map/ppermute | solution.py:16
  7.0 0.0 collective-permute-start.6
  7.0 0.1 fusion
  7.1 0.0 copy-done
  7.1 0.1 convert_reduce_fusion
  7.2 0.1 multiply_reduce_fusion
  7.3 1.2 %shard_map.51 = (bf16[512,128]{1,0:T(8,128)(2,1)S(1)}, bf16[512,128]{1,0:T(8,128)(2,1)S(1)}, bf16[512,128]{1,0:T(8,128)(2,1)S(1)}) custom-call(s32[1]{0:T(128)} %bitcast.me_ref, f32[8,512,128]{2,1,0:T(8,128)} %bitcast.16), custom_call_target="tpu_custom_call" | custom-call | tf_op jit(solution)/shard_map/pallas_call | solution.py:45
  8.4 0.1 reshape.55
  8.5 0.1 fusion.1
  8.6 0.0 collective-permute-done.refs_1_
  8.6 1.7 %collective-permute-start.1 = (bf16[512,128]{1,0:T(8,128)(2,1)S(1)}, bf16[512,128]{1,0:T(8,128)(2,1)S(1)}, u32[]{:S(2)}, u32[]{:S(2)}) collective-permute-start(bf16[512,128]{1,0:T(8,128)(2,1)S(1)} %get-tuple-element.14), channel_id=1, source_target_pairs={{0,8},{4,12},{8,0},{12,4},{16,24},{20,28},{24,16},{28,20},{1,9},{5... | collective-permute-start | bytes 393224 | tf_op jit(solution)/shard_map/ppermute | solution.py:16
  10.3 0.0 collective-permute-done.2.refs_3_
  10.3 1.5 %collective-permute-start.3 = (bf16[512,128]{1,0:T(8,128)(2,1)S(1)}, bf16[512,128]{1,0:T(8,128)(2,1)S(1)}, u32[]{:S(2)}, u32[]{:S(2)}) collective-permute-start(bf16[512,128]{1,0:T(8,128)(2,1)S(1)} %get-tuple-element.16), channel_id=1, source_target_pairs={{0,16},{4,20},{8,24},{12,28},{16,0},{20,4},{24,8},{28,12},{1,17},{... | collective-permute-start | bytes 393224 | tf_op jit(solution)/shard_map/ppermute | solution.py:16
  11.8 1.9 %collective-permute-done.4.refs_5_ = bf16[512,128]{1,0:T(8,128)(2,1)S(1)} collective-permute-done((bf16[512,128]{1,0:T(8,128)(2,1)S(1)}, bf16[512,128]{1,0:T(8,128)(2,1)S(1)}, u32[]{:S(2)}, u32[]{:S(2)}) %collective-permute-start.4) | collective-permute-done | bytes 131104 | tf_op jit(solution)/shard_map/ppermute | solution.py:16
  13.7 0.0 collective-permute-start.5
  13.7 0.1 pad_maximum_fusion.weights_ref
  13.8 0.0 collective-permute-done.6.refs_7_
  13.8 1.8 %collective-permute-done.1.refs_2_ = bf16[512,128]{1,0:T(8,128)(2,1)S(1)} collective-permute-done((bf16[512,128]{1,0:T(8,128)(2,1)S(1)}, bf16[512,128]{1,0:T(8,128)(2,1)S(1)}, u32[]{:S(2)}, u32[]{:S(2)}) %collective-permute-start.1) | collective-permute-done | bytes 131104 | tf_op jit(solution)/shard_map/ppermute | solution.py:16
  15.6 1.3 %collective-permute-done.3.refs_4_ = bf16[512,128]{1,0:T(8,128)(2,1)S(1)} collective-permute-done((bf16[512,128]{1,0:T(8,128)(2,1)S(1)}, bf16[512,128]{1,0:T(8,128)(2,1)S(1)}, u32[]{:S(2)}, u32[]{:S(2)}) %collective-permute-start.3) | collective-permute-done | bytes 131104 | tf_op jit(solution)/shard_map/ppermute | solution.py:16
  16.9 3.7 %collective-permute-done.5.refs_6_ = bf16[512,128]{1,0:T(8,128)(2,1)S(1)} collective-permute-done((bf16[512,128]{1,0:T(8,128)(2,1)S(1)}, bf16[512,128]{1,0:T(8,128)(2,1)S(1)}, u32[]{:S(2)}, u32[]{:S(2)}) %collective-permute-start.5) | collective-permute-done | bytes 131104 | tf_op jit(solution)/shard_map/ppermute | solution.py:16
  20.6 1.7 %scores.1 = f32[32,1,128]{2,1,0:T(1,128)} custom-call(f32[72,128]{1,0:T(8,128)S(1)} %pad_maximum_fusion.weights_ref, bf16[512,128]{1,0:T(8,128)(2,1)S(1)} %get-tuple-element.12.refs_0_, bf16[512,128]{1,0:T(8,128)(2,1)S(1)} %collective-permute-done.refs_1_, bf16[512,128]{1,0:T(8,128)(2,1)S(1)} %collective-permute-done.1.refs_2_, ...), custom_call_target="tpu_custom_call" | custom-call | tf_op jit(solution)/shard_map/scores/pallas_call | solution.py:91
  22.3 4.7 %all-to-all-start = ((f32[32,1,128]{2,1,0:T(1,128)}), f32[32,1,128]{2,1,0:T(1,128)S(1)}, u32[]{:S(2)}, u32[]{:S(2)}) async-start(f32[32,1,128]{2,1,0:T(1,128)} %scores.1), calls=%async_computation | async-start | bytes 32768 | tf_op jit(solution)/shard_map/all_to_all | solution.py:155
  27.6 6.5 %all-to-all-done = f32[32,1,128]{2,1,0:T(1,128)S(1)} async-done(((f32[32,1,128]{2,1,0:T(1,128)}), f32[32,1,128]{2,1,0:T(1,128)S(1)}, u32[]{:S(2)}, u32[]{:S(2)}) %all-to-all-start) | async-done | bytes 16416 | tf_op jit(solution)/shard_map/all_to_all | solution.py:155
  34.1 0.1 reduce_sum.31
  34.1 0.0 collective-permute-done.7
  34.1 0.1 broadcast_select_fusion
  34.3 0.6 %collective-permute-start.10 = (bf16[512,128]{1,0:T(8,128)(2,1)S(1)}, bf16[512,128]{1,0:T(8,128)(2,1)S(1)}, u32[]{:S(2)}, u32[]{:S(2)}) collective-permute-start(bf16[512,128]{1,0:T(8,128)(2,1)S(1)} %get-tuple-element.22), channel_id=1, source_target_pairs={{0,24},{4,28},{8,16},{12,20},{16,8},{20,12},{24,0},{28,4},{1,25},{... | collective-permute-start | bytes 393224 | tf_op jit(solution)/shard_map/ppermute | solution.py:16
  34.9 1.5 %collective-permute-start.8 = (bf16[512,128]{1,0:T(8,128)(2,1)S(1)}, bf16[512,128]{1,0:T(8,128)(2,1)S(1)}, u32[]{:S(2)}, u32[]{:S(2)}) collective-permute-start(bf16[512,128]{1,0:T(8,128)(2,1)S(1)} %get-tuple-element.24), channel_id=1, source_target_pairs={{0,8},{4,12},{8,0},{12,4},{16,24},{20,28},{24,16},{28,20},{1,9},{5... | collective-permute-start | bytes 393224 | tf_op jit(solution)/shard_map/ppermute | solution.py:16
  36.4 1.4 %collective-permute-start.9 = (bf16[512,128]{1,0:T(8,128)(2,1)S(1)}, bf16[512,128]{1,0:T(8,128)(2,1)S(1)}, u32[]{:S(2)}, u32[]{:S(2)}) collective-permute-start(bf16[512,128]{1,0:T(8,128)(2,1)S(1)} %get-tuple-element.23), channel_id=1, source_target_pairs={{0,16},{4,20},{8,24},{12,28},{16,0},{20,4},{24,8},{28,12},{1,17},{... | collective-permute-start | bytes 393224 | tf_op jit(solution)/shard_map/ppermute | solution.py:16
  37.8 0.5 %slice_bitcast_fusion.4 = f32[8]{0:T(128)} fusion(f32[1,128]{1,0:T(1,128)S(1)} %bitcast.18), kind=kLoop, calls=%fused_computation.12 | loop fusion | bytes 64 | tf_op jit(solution)/shard_map/squeeze | solution.py:158
  38.3 3.3 %collective-permute-done.10.refs_11_ = bf16[512,128]{1,0:T(8,128)(2,1)S(1)} collective-permute-done((bf16[512,128]{1,0:T(8,128)(2,1)S(1)}, bf16[512,128]{1,0:T(8,128)(2,1)S(1)}, u32[]{:S(2)}, u32[]{:S(2)}) %collective-permute-start.10) | collective-permute-done | bytes 131104 | tf_op jit(solution)/shard_map/ppermute | solution.py:16
  41.6 1.7 %collective-permute-done.8.refs_9_ = bf16[512,128]{1,0:T(8,128)(2,1)S(1)} collective-permute-done((bf16[512,128]{1,0:T(8,128)(2,1)S(1)}, bf16[512,128]{1,0:T(8,128)(2,1)S(1)}, u32[]{:S(2)}, u32[]{:S(2)}) %collective-permute-start.8) | collective-permute-done | bytes 131104 | tf_op jit(solution)/shard_map/ppermute | solution.py:16
  43.4 0.9 %collective-permute-done.9.refs_10_ = bf16[512,128]{1,0:T(8,128)(2,1)S(1)} collective-permute-done((bf16[512,128]{1,0:T(8,128)(2,1)S(1)}, bf16[512,128]{1,0:T(8,128)(2,1)S(1)}, u32[]{:S(2)}, u32[]{:S(2)}) %collective-permute-start.9) | collective-permute-done | bytes 131104 | tf_op jit(solution)/shard_map/ppermute | solution.py:16
  44.2 0.8 %merge.1 = f32[512,128]{1,0:T(8,128)} custom-call(s32[1]{0:T(128)S(6)} %xor.20.place_ref, bf16[512,128]{1,0:T(8,128)(2,1)S(1)} %get-tuple-element.12.refs_0_, bf16[512,128]{1,0:T(8,128)(2,1)S(1)} %collective-permute-done.refs_1_, bf16[512,128]{1,0:T(8,128)(2,1)S(1)} %collective-permute-done.1.refs_2_, bf16[512,128]{1,0:T(8,128)(2,1)S(1)} %collective-permute-done.2.refs_3_, ...), custom_call_target="tpu_custom_call" | custom-call | tf_op jit(solution)/shard_map/merge/pallas_call | solution.py:111
  (3 shorter events, 0.0 us)
Async XLA Ops:
  0.6 6.5 %copy-start = (s32[8,3]{0,1:T(4,128)S(1)}, s32[8,3]{0,1:T(4,128)}, u32[]{:S(2)}) copy-start(s32[8,3]{0,1:T(4,128)} %param.4) | copy-start | bytes 292
  2.3 31.9 %collective-permute-start.7 = (bf16[4,512,128]{2,1,0:T(8,128)(2,1)S(1)}, bf16[4,512,128]{2,1,0:T(8,128)(2,1)}, u32[]{:S(2)}, u32[]{:S(2)}) collective-permute-start(bf16[4,512,128]{2,1,0:T(8,128)(2,1)S(1)} %get-tuple-element.21), channel_id=1, source_target_pairs={{0,4},{4,0},{8,12},{12,8},{16,20},{20,16},{24,28},{28,24},{1,5},{5... | collective-permute-start | bytes 1572872 | tf_op jit(solution)/shard_map/ppermute | solution.py:16
  2.8 5.8 %collective-permute-start = (bf16[512,128]{1,0:T(8,128)(2,1)S(1)}, bf16[512,128]{1,0:T(8,128)(2,1)S(1)}, u32[]{:S(2)}, u32[]{:S(2)}) collective-permute-start(bf16[512,128]{1,0:T(8,128)(2,1)S(1)} %get-tuple-element.13), channel_id=1, source_target_pairs={{0,4},{4,0},{8,12},{12,8},{16,20},{20,16},{24,28},{28,24},{1,5},{5... | collective-permute-start | bytes 393224 | tf_op jit(solution)/shard_map/ppermute | solution.py:16
  2.9 7.4 %collective-permute-start.2 = (bf16[512,128]{1,0:T(8,128)(2,1)S(1)}, bf16[512,128]{1,0:T(8,128)(2,1)S(1)}, u32[]{:S(2)}, u32[]{:S(2)}) collective-permute-start(bf16[512,128]{1,0:T(8,128)(2,1)S(1)} %get-tuple-element.15), channel_id=1, source_target_pairs={{0,12},{4,8},{8,4},{12,0},{16,28},{20,24},{24,20},{28,16},{1,13},{... | collective-permute-start | bytes 393224 | tf_op jit(solution)/shard_map/ppermute | solution.py:16
  5.5 8.3 %collective-permute-start.4 = (bf16[512,128]{1,0:T(8,128)(2,1)S(1)}, bf16[512,128]{1,0:T(8,128)(2,1)S(1)}, u32[]{:S(2)}, u32[]{:S(2)}) collective-permute-start(bf16[512,128]{1,0:T(8,128)(2,1)S(1)} %get-tuple-element.17), channel_id=1, source_target_pairs={{0,20},{4,16},{8,28},{12,24},{16,4},{20,0},{24,12},{28,8},{1,21},{... | collective-permute-start | bytes 393224 | tf_op jit(solution)/shard_map/ppermute | solution.py:16
  7.0 6.8 %collective-permute-start.6 = (bf16[512,128]{1,0:T(8,128)(2,1)S(1)}, bf16[512,128]{1,0:T(8,128)(2,1)S(1)}, u32[]{:S(2)}, u32[]{:S(2)}) collective-permute-start(bf16[512,128]{1,0:T(8,128)(2,1)S(1)} %get-tuple-element.19), channel_id=1, source_target_pairs={{0,28},{4,24},{8,20},{12,16},{16,12},{20,8},{24,4},{28,0},{1,29},{... | collective-permute-start | bytes 393224 | tf_op jit(solution)/shard_map/ppermute | solution.py:16
  8.6 7.0 %collective-permute-start.1 = (bf16[512,128]{1,0:T(8,128)(2,1)S(1)}, bf16[512,128]{1,0:T(8,128)(2,1)S(1)}, u32[]{:S(2)}, u32[]{:S(2)}) collective-permute-start(bf16[512,128]{1,0:T(8,128)(2,1)S(1)} %get-tuple-element.14), channel_id=1, source_target_pairs={{0,8},{4,12},{8,0},{12,4},{16,24},{20,28},{24,16},{28,20},{1,9},{5... | collective-permute-start | bytes 393224 | tf_op jit(solution)/shard_map/ppermute | solution.py:16
  10.3 6.6 %collective-permute-start.3 = (bf16[512,128]{1,0:T(8,128)(2,1)S(1)}, bf16[512,128]{1,0:T(8,128)(2,1)S(1)}, u32[]{:S(2)}, u32[]{:S(2)}) collective-permute-start(bf16[512,128]{1,0:T(8,128)(2,1)S(1)} %get-tuple-element.16), channel_id=1, source_target_pairs={{0,16},{4,20},{8,24},{12,28},{16,0},{20,4},{24,8},{28,12},{1,17},{... | collective-permute-start | bytes 393224 | tf_op jit(solution)/shard_map/ppermute | solution.py:16
  13.7 6.9 %collective-permute-start.5 = (bf16[512,128]{1,0:T(8,128)(2,1)S(1)}, bf16[512,128]{1,0:T(8,128)(2,1)S(1)}, u32[]{:S(2)}, u32[]{:S(2)}) collective-permute-start(bf16[512,128]{1,0:T(8,128)(2,1)S(1)} %get-tuple-element.18), channel_id=1, source_target_pairs={{0,24},{4,28},{8,16},{12,20},{16,8},{20,12},{24,0},{28,4},{1,25},{... | collective-permute-start | bytes 393224 | tf_op jit(solution)/shard_map/ppermute | solution.py:16
  22.3 11.8 %all-to-all-start = ((f32[32,1,128]{2,1,0:T(1,128)}), f32[32,1,128]{2,1,0:T(1,128)S(1)}, u32[]{:S(2)}, u32[]{:S(2)}) async-start(f32[32,1,128]{2,1,0:T(1,128)} %scores.1), calls=%async_computation | async-start | bytes 32768 | tf_op jit(solution)/shard_map/all_to_all | solution.py:155
  34.3 7.4 %collective-permute-start.10 = (bf16[512,128]{1,0:T(8,128)(2,1)S(1)}, bf16[512,128]{1,0:T(8,128)(2,1)S(1)}, u32[]{:S(2)}, u32[]{:S(2)}) collective-permute-start(bf16[512,128]{1,0:T(8,128)(2,1)S(1)} %get-tuple-element.22), channel_id=1, source_target_pairs={{0,24},{4,28},{8,16},{12,20},{16,8},{20,12},{24,0},{28,4},{1,25},{... | collective-permute-start | bytes 393224 | tf_op jit(solution)/shard_map/ppermute | solution.py:16
  34.9 8.5 %collective-permute-start.8 = (bf16[512,128]{1,0:T(8,128)(2,1)S(1)}, bf16[512,128]{1,0:T(8,128)(2,1)S(1)}, u32[]{:S(2)}, u32[]{:S(2)}) collective-permute-start(bf16[512,128]{1,0:T(8,128)(2,1)S(1)} %get-tuple-element.24), channel_id=1, source_target_pairs={{0,8},{4,12},{8,0},{12,4},{16,24},{20,28},{24,16},{28,20},{1,9},{5... | collective-permute-start | bytes 393224 | tf_op jit(solution)/shard_map/ppermute | solution.py:16
  36.4 7.9 %collective-permute-start.9 = (bf16[512,128]{1,0:T(8,128)(2,1)S(1)}, bf16[512,128]{1,0:T(8,128)(2,1)S(1)}, u32[]{:S(2)}, u32[]{:S(2)}) collective-permute-start(bf16[512,128]{1,0:T(8,128)(2,1)S(1)} %get-tuple-element.23), channel_id=1, source_target_pairs={{0,16},{4,20},{8,24},{12,28},{16,0},{20,4},{24,8},{28,12},{1,17},{... | collective-permute-start | bytes 393224 | tf_op jit(solution)/shard_map/ppermute | solution.py:16
